TPU v7x, 256 devices: a whole 4x4x8 slice. The times are simulated.
256 devices in a mesh: act: 64 (over x, z, core), rep: 4 (over y).
Axes of the slice: x: 4, y: 4, z: 8, core: 2. Of those that a mesh axis runs over, the one named last changes fastest.
Arguments:
- estimated_returns: float32 [512, 131072], P('act', 'rep'), may hold values from -1000 to 1000
- chosen_move_ids: int32 [512, 131072], P('act', 'rep'), may hold values from 0 to 17
- previous_eta: float32 [1], replicated, may hold values from 0.3 to 3
- trust_region_epsilon: float32 [1], replicated, may hold values from 0.02 to 1
Outputs:
- sample_importance: float32 [512, 131072], P('act', 'rep')
- goal_distribution: float32 [18, 131072], P(None, ('rep', 'act'))
- new_temperature: float32 [1], replicated
All inputs are finite; a program needn't handle non-finite values.
Results may differ from a plain program's by a relative error of at most 0.0003.
Values sent between devices are 32-bit elements; how exact they have to be, the bound alone decides.
No kernel may reach another device: no remote copies, remote signals or barrier semaphores. Data moves between devices by JAX's collectives and lax.ppermute only.
A program may use at most 64 MiB of HBM per device.

v0:
```python
import jax
import jax.numpy as jnp
from jax import lax
from jax.sharding import Mesh
from jax.sharding import PartitionSpec as P

NACT = 18
ITERS = 3
ACT = ("act_0", "act_1", "act_2")
REP_ACT = ("rep", "act_0", "act_1", "act_2")


def cut_along(shard, dim, peers):
    shape = shard.shape
    blocks = shard.reshape(*shape[:dim], peers, shape[dim] // peers, *shape[dim + 1 :])
    return jnp.moveaxis(blocks, dim, 0)


def sum_at_owner(shard, axis, dim):
    blocks = cut_along(shard, dim, lax.axis_size(axis))
    arrived = lax.all_to_all(blocks, axis, split_axis=0, concat_axis=0, tiled=True)
    return arrived.sum(axis=0)


def sum_in_two_steps(shard, axes, dim):
    far, near = axes
    own = sum_at_owner(cut_along(shard, dim, lax.axis_size(far)), near, dim + 1)
    return jnp.sum(lax.all_to_all(own, far, 0, 0, tiled=True), axis=0)


def copy_for_each(shard, axis):
    copies = jnp.broadcast_to(shard, (lax.axis_size(axis), *shard.shape))
    return lax.all_to_all(copies, axis, split_axis=0, concat_axis=0, tiled=True)


def over_copies(shard, axis):
    everything = copy_for_each(shard, axis)
    return jnp.sum(everything, axis=0)


def by_axis(shard, axes):
    far, near = axes
    return over_copies(over_copies(shard, near), far)


def together(arrays, axis):
    ends = [0]
    for a in arrays:
        ends.append(ends[-1] + a.size)
    total = by_axis(jnp.concatenate([a.ravel() for a in arrays]), axis)
    return tuple((total[b:e].reshape(a.shape) for a, b, e in zip(arrays, ends, ends[1:])))


def summary_figures(centered_returns, lagrange_eta):
    exponential_term = jnp.exp(centered_returns / lagrange_eta)
    partition_total = jnp.sum(exponential_term, axis=0)
    leading_part = jnp.sum(exponential_term * centered_returns, axis=0)
    trailing_part = jnp.sum(exponential_term * centered_returns * centered_returns, axis=0)
    return (exponential_term, partition_total, leading_part, trailing_part)


def within_situation(partition_total, leading_part, trailing_part, lagrange_eta, move_draws):
    entropy_gap = (
        leading_part / (partition_total * lagrange_eta)
        - jnp.log(partition_total)
        + jnp.log(jnp.float32(move_draws))
    )
    mean_first = leading_part / partition_total
    spread = trailing_part / partition_total - mean_first * mean_first
    return (jnp.sum(entropy_gap), jnp.sum(spread))


def gradient_step(lagrange_eta, ceiling_term, aggregate_relative_entropy, aggregate_deviation):
    change_amount = (
        (ceiling_term - aggregate_relative_entropy)
        * lagrange_eta
        / (1.0 + aggregate_deviation / lagrange_eta)
    )
    return lagrange_eta * jnp.exp(-jnp.tanh(change_amount))


def per_action(probs, ids_block):
    return jnp.stack([jnp.sum(jnp.where(ids_block == k, probs, 0.0), axis=0) for k in range(NACT)])


def scatter_target(probs, ids_block):
    return sum_in_two_steps(per_action(probs, ids_block), (("act_0", "act_1"), "act_2"), 1)


def on_device(estimated_returns, chosen_move_ids, previous_eta, trust_region_epsilon):
    lagrange_eta = previous_eta[0]
    ceiling_term = trust_region_epsilon[0]
    move_draws = estimated_returns.shape[0] * lax.axis_size(ACT)
    q_rows = lax.all_to_all(estimated_returns, ACT, split_axis=1, concat_axis=0, tiled=True)
    tally_number = q_rows.shape[1] * lax.axis_size(ACT) * lax.axis_size("rep")
    centered_returns = q_rows - jnp.max(q_rows, axis=0, keepdims=True)
    for step in range(ITERS):
        exponential_term, partition_total, leading_part, trailing_part = summary_figures(
            centered_returns, lagrange_eta
        )
        shard_divergence, shard_value_spread = within_situation(
            partition_total, leading_part, trailing_part, lagrange_eta, move_draws
        )
        aggregate_relative_entropy, aggregate_deviation = together(
            (shard_divergence, shard_value_spread), (("act_0", "act_1"), ("act_2", "rep"))
        )
        lagrange_eta = gradient_step(
            lagrange_eta,
            ceiling_term,
            aggregate_relative_entropy / tally_number,
            aggregate_deviation / tally_number,
        )
    exponential_term, partition_total, leading_part, trailing_part = summary_figures(
        centered_returns, lagrange_eta
    )
    probs_rows = exponential_term / partition_total
    sample_importance = lax.all_to_all(
        move_draws * probs_rows, ACT, split_axis=0, concat_axis=1, tiled=True
    )
    goal_distribution = scatter_target(sample_importance / jnp.float32(move_draws), chosen_move_ids)
    return (sample_importance, goal_distribution, jnp.reshape(lagrange_eta, (1,)))


def solution(mesh):
    split = Mesh(
        mesh.devices.reshape(4, 8, 2, mesh.shape["rep"]), ("act_0", "act_1", "act_2", "rep")
    )
    placed = (P(ACT, "rep"), P(ACT, "rep"), P(), P())
    return jax.shard_map(
        on_device,
        mesh=split,
        in_specs=placed,
        out_specs=(P(ACT, "rep"), P(None, REP_ACT), P()),
        check_vma=False,
    )
```

profile of v0, /device:TPU:32, one launch (start us, length us, event | category | flops | bytes accessed | tf_op | source)
XLA Modules:
  0.0 227.9 jit_solution(15470701140509389967)
XLA Ops:
  0.6 11.6 %all-to-all-start = ((f32[8,64,512]{2,0,1:T(8,128)}), f32[8,64,512]{2,0,1:T(8,128)S(1)}, u32[]{:S(2)}, u32[]{:S(2)}) async-start(f32[8,64,512]{2,0,1:T(8,128)} %bitcast.90), calls=%async_computation | async-start | bytes 2097152 | tf_op jit(solution)/shard_map/all_to_all | solution.py:94
  12.9 27.2 %all-to-all-done = f32[8,64,512]{2,0,1:T(8,128)S(1)} async-done(((f32[8,64,512]{2,0,1:T(8,128)}), f32[8,64,512]{2,0,1:T(8,128)S(1)}, u32[]{:S(2)}, u32[]{:S(2)}) %all-to-all-start) | async-done | bytes 1048608 | tf_op jit(solution)/shard_map/all_to_all | solution.py:94
  40.5 0.6 add_reduce_fusion.2
  41.2 1.4 pad_maximum_fusion
  42.5 9.5 %all_to_all.75 = f32[8,1,2]{2,1,0:T(1,128)S(1)} all-to-all(f32[8,1,2]{2,1,0:T(1,128)S(1)} %broadcast_in_dim.41), channel_id=1, replica_groups=mesh['act_0'=4,'act_1'=8,'act_2'=2,'rep'=4] {'act_2','rep'}, dimensions={0} | all-to-all | bytes 128 | tf_op jit(solution)/shard_map/all_to_all | solution.py:33
  52.1 0.6 broadcast_in_dim.42
  52.7 6.5 %all-to-all-start.2 = ((f32[32,1,2]{2,1,0:T(1,128)}), f32[32,1,2]{2,1,0:T(1,128)S(1)}, u32[]{:S(2)}, u32[]{:S(2)}) async-start(f32[32,1,2]{2,1,0:T(1,128)} %broadcast_in_dim.42), calls=%async_computation.2 | async-start | bytes 32768 | tf_op jit(solution)/shard_map/all_to_all | solution.py:33
  59.8 7.9 %all-to-all-done.2 = f32[32,1,2]{2,1,0:T(1,128)S(1)} async-done(((f32[32,1,2]{2,1,0:T(1,128)}), f32[32,1,2]{2,1,0:T(1,128)S(1)}, u32[]{:S(2)}, u32[]{:S(2)}) %all-to-all-start.2) | async-done | bytes 288 | tf_op jit(solution)/shard_map/all_to_all | solution.py:33
  70.8 1.4 pad_maximum_fusion.1
  72.2 7.6 %all_to_all.76 = f32[8,1,2]{2,1,0:T(1,128)S(1)} all-to-all(f32[8,1,2]{2,1,0:T(1,128)S(1)} %broadcast_in_dim.43), channel_id=1, replica_groups=mesh['act_0'=4,'act_1'=8,'act_2'=2,'rep'=4] {'act_2','rep'}, dimensions={0} | all-to-all | bytes 128 | tf_op jit(solution)/shard_map/all_to_all | solution.py:33
  79.8 12.8 %all_to_all.77 = f32[32,1,2]{2,1,0:T(1,128)S(1)} all-to-all(f32[32,1,2]{2,1,0:T(1,128)S(1)} %broadcast_in_dim.44), channel_id=1, replica_groups=mesh['act_0'=4,'act_1'=8,'act_2'=2,'rep'=4] {'act_0','act_1'}, dimensions={0} | all-to-all | bytes 512 | tf_op jit(solution)/shard_map/all_to_all | solution.py:33
  95.7 1.4 pad_maximum_fusion.2
  97.1 7.6 %all_to_all.78 = f32[8,1,2]{2,1,0:T(1,128)S(1)} all-to-all(f32[8,1,2]{2,1,0:T(1,128)S(1)} %broadcast_in_dim.45), channel_id=1, replica_groups=mesh['act_0'=4,'act_1'=8,'act_2'=2,'rep'=4] {'act_2','rep'}, dimensions={0} | all-to-all | bytes 128 | tf_op jit(solution)/shard_map/all_to_all | solution.py:33
  104.7 12.8 %all_to_all.79 = f32[32,1,2]{2,1,0:T(1,128)S(1)} all-to-all(f32[32,1,2]{2,1,0:T(1,128)S(1)} %broadcast_in_dim.46), channel_id=1, replica_groups=mesh['act_0'=4,'act_1'=8,'act_2'=2,'rep'=4] {'act_0','act_1'}, dimensions={0} | all-to-all | bytes 512 | tf_op jit(solution)/shard_map/all_to_all | solution.py:33
  120.0 32.8 %all_to_all.80 = f32[64,8,512]{2,1,0:T(8,128)S(1)} all-to-all(f32[64,8,512]{2,1,0:T(8,128)S(1)} %divide_multiply_fusion), channel_id=1, replica_groups=mesh['act_0'=4,'act_1'=8,'act_2'=2,'rep'=4] {'act_0','act_1','act_2'}, dimensions={0} | all-to-all | bytes 2097152 | tf_op jit(solution)/shard_map/all_to_all | solution.py:117
  152.8 10.5 %select_reduce_fusion = (f32[32768]{0:T(1024)S(1)}, f32[32768]{0:T(1024)S(1)}, f32[32768]{0:T(1024)S(1)}, f32[32768]{0:T(1024)S(1)}, f32[32768]{0:T(1024)S(1)}, ...) fusion(s32[8,32768]{1,0:T(8,128)S(1)} %copy-done.1, ...), kind=kLoop, calls=%fused_computation.17 | loop fusion | flops 13828096 | bytes 4456448 | tf_op jit(solution)/shard_map/reduce_sum | solution.py:83
  164.2 1.4 copy-done
  165.7 3.3 %reshape.176 = f32[32,18,2,512]{3,2,0,1:T(2,128)S(1)} reshape(f32[32,18,1024]{2,0,1:T(8,128)} %bitcast.89) | data formatting | bytes 4718592 | tf_op jit(solution)/shard_map/reshape | solution.py:15
  169.5 5.6 %all_to_all.81 = f32[2,32,18,512]{3,1,2,0:T(8,128)S(1)} all-to-all(f32[2,32,18,512]{3,1,2,0:T(8,128)S(1)} %copy.19), channel_id=1, replica_groups=mesh['act_0'=4,'act_1'=8,'act_2'=2,'rep'=4] {'act_2'}, dimensions={0} | all-to-all | bytes 4718592 | tf_op jit(solution)/shard_map/all_to_all | solution.py:21
  175.1 1.3 reduce_sum.418
  176.4 2.0 copy.20
  178.4 46.7 %all_to_all.82 = f32[32,18,512]{2,1,0:T(8,128)S(1)} all-to-all(f32[32,18,512]{2,1,0:T(8,128)S(1)} %copy.20), channel_id=1, replica_groups=mesh['act_0'=4,'act_1'=8,'act_2'=2,'rep'=4] {'act_0','act_1'}, dimensions={0} | all-to-all | bytes 2359296 | tf_op jit(solution)/shard_map/all_to_all | solution.py:28
  225.1 0.7 reduce_sum.419
  225.8 1.0 copy.53
  (62 shorter events, 6.0 us)
Async XLA Ops:
  0.6 39.5 %all-to-all-start = ((f32[8,64,512]{2,0,1:T(8,128)}), f32[8,64,512]{2,0,1:T(8,128)S(1)}, u32[]{:S(2)}, u32[]{:S(2)}) async-start(f32[8,64,512]{2,0,1:T(8,128)} %bitcast.90), calls=%async_computation | async-start | bytes 2097152 | tf_op jit(solution)/shard_map/all_to_all | solution.py:94
  52.7 15.0 %all-to-all-start.2 = ((f32[32,1,2]{2,1,0:T(1,128)}), f32[32,1,2]{2,1,0:T(1,128)S(1)}, u32[]{:S(2)}, u32[]{:S(2)}) async-start(f32[32,1,2]{2,1,0:T(1,128)} %broadcast_in_dim.42), calls=%async_computation.2 | async-start | bytes 32768 | tf_op jit(solution)/shard_map/all_to_all | solution.py:33
  119.8 33.0 %copy-start.1 = (s32[8,32768]{1,0:T(8,128)S(1)}, s32[8,32768]{1,0:T(8,128)}, u32[]{:S(2)}) copy-start(s32[8,32768]{1,0:T(8,128)} %param.5) | copy-start | bytes 3145732
  164.2 1.4 copy-start
where the time goes:
time: 229 us; the launch traced here: 228 us
  blocking collectives  135 us (59%)
  waiting for transfers between devices  35.1 us (15%)
  other arithmetic  20.2 us (9%)
  starting transfers between devices  18.1 us (8%)
  local copies, waits for them, and re-layouts  11.3 us (5%)
  between operations  7.81 us (3%)
    all_to_all x5, blocking collectives, copy_for_each(): return lax.all_to_all(copies, axis, split_axis=0, concat_axis=0, tiled=True)  50.3 us
    all_to_all x1, blocking collectives, sum_in_two_steps(): return jnp.sum(lax.all_to_all(own, far, 0, 0, tiled=True), axis=0)  46.7 us
    all_to_all x1, blocking collectives, on_device(): lax.all_to_all(move_draws * probs_rows, ACT, split_axis=0, concat_axis=1,...  32.8 us
    all_to_all x1, waiting for transfers between devices, on_device(): lax.all_to_all(estimated_returns, ACT, split_axis=1, concat_axis=0, tiled...  27.2 us
    all_to_all x1, starting transfers between devices, on_device(): lax.all_to_all(estimated_returns, ACT, split_axis=1, concat_axis=0, tiled...  11.6 us
    reduce_sum x1, other arithmetic, per_action(): jnp.sum(jnp.where(ids_block == k, probs, 0.0), axis=0)  10.5 us
    all_to_all x1, waiting for transfers between devices, copy_for_each(): return lax.all_to_all(copies, axis, split_axis=0, concat_axis=0, tiled=True)  7.92 us
    all_to_all x1, starting transfers between devices, copy_for_each(): return lax.all_to_all(copies, axis, split_axis=0, concat_axis=0, tiled=True)  6.46 us
  transfers between devices with their start and end apart: 2, of which 2 were waited for; matrix products, arithmetic and copies ran while one was open for 0% of the time, Pallas kernels for 0%

commit v1 on v0

v1 whole, which is shorter than its diff:
```python
import functools
import jax
import jax.numpy as jnp
from jax import lax
from jax.experimental import pallas as pl
from jax.experimental.pallas import tpu as pltpu
from jax.sharding import PartitionSpec as P

NACT = 18
ITERS = 3
LANES = 128
ALL = ("rep", "act")
VMEM = pl.BlockSpec(memory_space=pltpu.VMEM)
SMEM = pl.BlockSpec(memory_space=pltpu.SMEM)
PARAMS = pltpu.CompilerParams(vmem_limit_bytes=8 * 1024 * 1024)


def call(body, out_shape, name, n_smem, n_vmem, flops=1_000_000):
    n_out = len(out_shape) if isinstance(out_shape, (tuple, list)) else None
    return pl.pallas_call(
        body,
        out_shape=out_shape,
        in_specs=[SMEM] * n_smem + [VMEM] * n_vmem,
        out_specs=VMEM if n_out is None else [VMEM] * n_out,
        compiler_params=PARAMS,
        cost_estimate=pl.CostEstimate(flops=flops, bytes_accessed=2_000_000, transcendentals=262_144),
        name=name,
    )


def partial_sums(q_ref, top, eta, samples):
    blocks, rows, states = q_ref.shape
    inverse = jnp.broadcast_to((1.0 / eta)[:, :1], (rows, states))
    top_rows = jnp.broadcast_to(top, (rows, states))

    def step(i, sums):
        z, c1, c2 = sums
        shifted = q_ref[i] - top_rows
        expo = jnp.exp(shifted * inverse)
        first = expo * shifted
        return z + expo, c1 + first, c2 + first * shifted

    zero = jnp.zeros((rows, states), jnp.float32)
    z, c1, c2 = lax.fori_loop(0, blocks, step, (zero, zero, zero), unroll=8)
    z, c1, c2 = (jnp.sum(v, axis=0, keepdims=True) for v in (z, c1, c2))
    mean = c1 / z
    kl = mean * inverse[:1] - jnp.log(z) + jnp.log(jnp.float32(samples))
    spread = c2 / z - mean * mean
    lane = lax.broadcasted_iota(jnp.int32, (1, LANES), 1)
    kl_sum = jnp.sum(kl, axis=1, keepdims=True)
    spread_sum = jnp.sum(spread, axis=1, keepdims=True)
    return jnp.where(lane == 0, kl_sum, jnp.where(lane == 1, spread_sum, 0.0))


def next_eta(gathered_ref, eta, eps, states):
    total = jnp.sum(gathered_ref[...], axis=0) * jnp.float32(1.0 / states)
    divergence = jnp.broadcast_to(total[:, 0:1], eta.shape)
    deviation = jnp.broadcast_to(total[:, 1:2], eta.shape)
    change = (eps - divergence) * eta / (1.0 + deviation / eta)
    return eta * jnp.exp(-jnp.tanh(change))


def row(scalar):
    return jnp.full((1, LANES), scalar, jnp.float32)


def first_body(samples, eta_ref, q_ref, top_ref, eta_out, part_ref):
    top8 = q_ref[0]
    top8 = lax.fori_loop(1, q_ref.shape[0], lambda i, m: jnp.maximum(m, q_ref[i]), top8)
    top = jnp.max(top8, axis=0, keepdims=True)
    top_ref[...] = top
    eta = row(eta_ref[0])
    eta_out[...] = eta
    part_ref[...] = jnp.broadcast_to(partial_sums(q_ref, top, eta, samples)[None], part_ref.shape)


def step_body(samples, states, eps_ref, q_ref, top_ref, eta_ref, gathered_ref, eta_out, part_ref):
    eta = next_eta(gathered_ref, eta_ref[...], row(eps_ref[0]), states)
    eta_out[...] = eta
    part_ref[...] = jnp.broadcast_to(partial_sums(q_ref, top_ref[...], eta, samples)[None], part_ref.shape)


def last_body(samples, states, eps_ref, q_ref, top_ref, eta_ref, gathered_ref, eta_out, back_ref):
    eta = next_eta(gathered_ref, eta_ref[...], row(eps_ref[0]), states)
    eta_out[...] = eta
    blocks, rows, width = q_ref.shape
    inverse = jnp.broadcast_to((1.0 / eta)[:, :1], (rows, width))
    top = top_ref[...]
    top_rows = jnp.broadcast_to(top, (rows, width))
    z = lax.fori_loop(
        0, blocks, lambda i, z: z + jnp.exp((q_ref[i] - top_rows) * inverse),
        jnp.zeros((rows, width), jnp.float32), unroll=8)
    scale = jnp.float32(samples) / jnp.sum(z, axis=0, keepdims=True)
    copies = back_ref.shape[0]
    back_ref[:, :, :width] = jnp.broadcast_to(top[None], (copies, 1, width))
    back_ref[:, :, width:] = jnp.broadcast_to(scale[None], (copies, 1, width))


def goal_body(samples, q_ref, ids_ref, back_ref, eta_ref, goal_ref):
    blocks, rows, width = q_ref.shape
    inverse = jnp.broadcast_to((1.0 / eta_ref[...])[:, :1], (rows, LANES))
    for tile in range(width // LANES):
        at = slice(tile * LANES, (tile + 1) * LANES)
        top_rows = jnp.broadcast_to(back_ref[0, :, at], (rows, LANES))
        scale = back_ref[0, :, width + tile * LANES : width + (tile + 1) * LANES] * jnp.float32(1.0 / samples)

        def step(i, sums):
            expo = jnp.exp((q_ref[i, :, at] - top_rows) * inverse)
            ids = ids_ref[i, :, at]
            return tuple(s + jnp.where(ids == k, expo, 0.0) for k, s in enumerate(sums))

        zero = jnp.zeros((rows, LANES), jnp.float32)
        sums = lax.fori_loop(0, blocks, step, (zero,) * NACT, unroll=2)
        for k, s in enumerate(sums):
            goal_ref[k : k + 1, at] = jnp.sum(s, axis=0, keepdims=True) * scale


def weights_body(eta_ref, x_ref, back_ref, out_ref):
    rows, width = x_ref.shape
    owners, _, both = back_ref.shape
    own = both // 2
    inverse = jnp.broadcast_to((1.0 / eta_ref[...])[:, :1], (rows, own))
    for j in range(owners):
        at = slice(j * own, (j + 1) * own)
        top = jnp.broadcast_to(back_ref[j, :, :own], (rows, own))
        scale = jnp.broadcast_to(back_ref[j, :, own:], (rows, own))
        out_ref[:, at] = jnp.exp((x_ref[:, at] - top) * inverse) * scale


def send(blocks, axis):
    return lax.all_to_all(blocks, axis, split_axis=0, concat_axis=0, tiled=True)


def on_device(estimated_returns, chosen_move_ids, previous_eta, trust_region_epsilon):
    peers = lax.axis_size("act")
    everyone = peers * lax.axis_size("rep")
    rows, width = estimated_returns.shape
    own = width // peers
    samples, states = rows * peers, width * lax.axis_size("rep")
    f32 = jnp.float32
    shape = jax.ShapeDtypeStruct

    def to_owner(v):
        return send(v.reshape(rows, peers, own).transpose(1, 0, 2), "act")

    q = to_owner(estimated_returns)
    ids = to_owner(chosen_move_ids)

    eta_shape, part_shape = shape((1, LANES), f32), shape((everyone, 1, LANES), f32)
    top, eta, part = call(
        functools.partial(first_body, samples), [shape((1, own), f32), eta_shape, part_shape], "first", 1, 1
    )(previous_eta, q)
    for _ in range(ITERS - 1):
        gathered = send(part, ALL)
        eta, part = call(
            functools.partial(step_body, samples, states), [eta_shape, part_shape], "step", 1, 4
        )(trust_region_epsilon, q, top, eta, gathered)
    gathered = send(part, ALL)
    eta, back = call(
        functools.partial(last_body, samples, states),
        [eta_shape, shape((peers, 1, 2 * own), f32)], "last", 1, 4,
    )(trust_region_epsilon, q, top, eta, gathered)
    everywhere = send(back, "act")
    goal = call(
        functools.partial(goal_body, samples), shape((NACT, own), f32), "goal", 0, 4, flops=20_000_000
    )(q, ids, back, eta)

    steps = 8
    weights = pl.pallas_call(
        weights_body,
        grid=(steps,),
        out_shape=shape((rows, width), f32),
        in_specs=[
            pl.BlockSpec((1, LANES), lambda i: (0, 0)),
            pl.BlockSpec((rows, width // steps), lambda i: (0, i)),
            pl.BlockSpec((peers // steps, 1, 2 * own), lambda i: (i, 0, 0)),
        ],
        out_specs=pl.BlockSpec((rows, width // steps), lambda i: (0, i)),
        compiler_params=PARAMS,
        cost_estimate=pl.CostEstimate(flops=1_000_000, bytes_accessed=2_000_000, transcendentals=262_144),
        name="weights",
    )(eta, estimated_returns, everywhere)
    return weights, goal, eta[0, :1]


def solution(mesh):
    placed = (P("act", "rep"), P("act", "rep"), P(), P())
    return jax.shard_map(
        on_device,
        mesh=mesh,
        in_specs=placed,
        out_specs=(P("act", "rep"), P(None, ALL), P()),
        check_vma=False,
    )
```

time: 229 us -> 160 us (0.70)
  blocking collectives: 135 us -> 37.2 us
  waiting for transfers between devices: 35.1 us -> 71.8 us
  other arithmetic: 20.2 us -> 0 us
  starting transfers between devices: 18.1 us -> 33.1 us
  Pallas kernels: 0 us -> 13.1 us
  local copies, waits for them, and re-layouts: 11.3 us -> 0.65 us
  between operations: 7.81 us -> 1.98 us
    all_to_all x8 -> x2, blocking collectives: 135 us -> 37.2 us  [send(): return lax.all_to_all(blocks, axis, split_axis=0, concat_axis=0, tiled=True)]
    all_to_all x2 -> x4, waiting for transfers between devices: 35.1 us -> 71.8 us  [send(): return lax.all_to_all(blocks, axis, split_axis=0, concat_axis=0, tiled=True)]
    reduce_sum x16 -> x0, other arithmetic: 15.8 us -> none  [the longest x1 10.5 us: per_action(): jnp.sum(jnp.where(ids_block == k, probs, 0.0), axis=0)]
    all_to_all x2 -> x4, starting transfers between devices: 18.1 us -> 33.1 us  [send(): return lax.all_to_all(blocks, axis, split_axis=0, concat_axis=0, tiled=True)]
    pallas_call x0 -> x6, Pallas kernels: none -> 13.1 us  [the longest x1 5.05 us: on_device(): call(functools.partial(goal_body, samples), shape((NACT, own), f32), 'goa...]
    concatenate x3 -> x0, other arithmetic: 4.1 us -> none  [together(): total = by_axis(jnp.concatenate([a.ravel() for a in arrays]), axis)]
    reshape x1 -> x0, local copies, waits for them, and re-layouts: 3.34 us -> none  [cut_along(): shard.reshape(*shape[:dim], peers, shape[dim] // peers, *shape[dim + 1:])]
  transfers between devices with their start and end apart: 2 -> 4, of which waited for: 2 -> 4; matrix products, arithmetic and copies ran while one was open for 0% -> 0% of each run, Pallas kernels for 0% -> 4%
where the time goes in v1:
time: 160 us; the launch traced here: 158 us
  waiting for transfers between devices  71.8 us (45%)
  blocking collectives  37.2 us (23%)
  starting transfers between devices  33.1 us (21%)
  Pallas kernels  13.1 us (8%)
  between operations  1.98 us (1%)
    all_to_all x4, waiting for transfers between devices, send(): return lax.all_to_all(blocks, axis, split_axis=0, concat_axis=0, tiled=True)  71.8 us
    all_to_all x2, blocking collectives, send(): return lax.all_to_all(blocks, axis, split_axis=0, concat_axis=0, tiled=True)  37.2 us
    all_to_all x4, starting transfers between devices, send(): return lax.all_to_all(blocks, axis, split_axis=0, concat_axis=0, tiled=True)  33.1 us
    pallas_call x1, Pallas kernels, on_device(): call(functools.partial(goal_body, samples), shape((NACT, own), f32), 'goa...  5.05 us
  transfers between devices with their start and end apart: 4, of which 4 were waited for; matrix products, arithmetic and copies ran while one was open for 0% of the time, Pallas kernels for 4%

profile of v1, /device:TPU:32, one launch (start us, length us, event | category | flops | bytes accessed | tf_op | source)
XLA Modules:
  0.0 157.9 jit_solution(9115704796173390318)
XLA Ops:
  0.6 11.6 %all-to-all-start = ((f32[64,8,512]{2,1,0:T(8,128)}), f32[64,8,512]{2,1,0:T(8,128)S(1)}, u32[]{:S(2)}, u32[]{:S(2)}) async-start(f32[64,8,512]{2,1,0:T(8,128)} %bitcast.8), calls=%async_computation | async-start | bytes 2097152 | tf_op jit(solution)/shard_map/all_to_all | solution.py:131
  12.9 27.2 %all-to-all-done.q_ref = f32[64,8,512]{2,1,0:T(8,128)S(1)} async-done(((f32[64,8,512]{2,1,0:T(8,128)}), f32[64,8,512]{2,1,0:T(8,128)S(1)}, u32[]{:S(2)}, u32[]{:S(2)}) %all-to-all-start) | async-done | bytes 1048608 | tf_op jit(solution)/shard_map/all_to_all | solution.py:131
  40.1 1.5 first.1
  41.6 9.7 %all-to-all-start.1 = ((f32[256,1,128]{2,1,0:T(1,128)}), f32[256,1,128]{2,1,0:T(1,128)S(1)}, u32[]{:S(2)}, u32[]{:S(2)}) async-start(f32[256,1,128]{2,1,0:T(1,128)} %get-tuple-element.14), calls=%async_computation.1 | async-start | bytes 262144 | tf_op jit(solution)/shard_map/all_to_all | solution.py:131
  51.9 12.1 %all-to-all-done.1.gathered_ref = f32[256,1,128]{2,1,0:T(1,128)S(1)} async-done(((f32[256,1,128]{2,1,0:T(1,128)}), f32[256,1,128]{2,1,0:T(1,128)S(1)}, u32[]{:S(2)}, u32[]{:S(2)}) %all-to-all-start.1) | async-done | bytes 131104 | tf_op jit(solution)/shard_map/all_to_all | solution.py:131
  64.0 1.0 step.2
  65.0 18.6 %all_to_all.30.gathered_ref = f32[256,1,128]{2,1,0:T(1,128)S(1)} all-to-all(f32[256,1,128]{2,1,0:T(1,128)S(1)} %get-tuple-element.16), channel_id=1, replica_groups=mesh['act'=64,'rep'=4] {'rep','act'}, dimensions={0} | all-to-all | bytes 262144 | tf_op jit(solution)/shard_map/all_to_all | solution.py:131
  83.6 1.0 step.3
  84.6 18.6 %all_to_all.31.gathered_ref = f32[256,1,128]{2,1,0:T(1,128)S(1)} all-to-all(f32[256,1,128]{2,1,0:T(1,128)S(1)} %get-tuple-element.18), channel_id=1, replica_groups=mesh['act'=64,'rep'=4] {'rep','act'}, dimensions={0} | all-to-all | bytes 262144 | tf_op jit(solution)/shard_map/all_to_all | solution.py:131
  103.2 5.0 %all-to-all-start.5 = ((s32[64,8,512]{2,1,0:T(8,128)}), s32[64,8,512]{2,1,0:T(8,128)S(1)}, u32[]{:S(2)}, u32[]{:S(2)}) async-start(s32[64,8,512]{2,1,0:T(8,128)} %bitcast.3), calls=%async_computation.5 | async-start | bytes 2097152 | tf_op jit(solution)/shard_map/all_to_all | solution.py:131
  108.2 1.4 last.1
  109.6 26.5 %all-to-all-done.5.ids_ref = s32[64,8,512]{2,1,0:T(8,128)S(1)} async-done(((s32[64,8,512]{2,1,0:T(8,128)}), s32[64,8,512]{2,1,0:T(8,128)S(1)}, u32[]{:S(2)}, u32[]{:S(2)}) %all-to-all-start.5) | async-done | bytes 1048608 | tf_op jit(solution)/shard_map/all_to_all | solution.py:131
  136.1 6.9 %all-to-all-start.4 = ((f32[64,1,1024]{2,1,0:T(1,128)}), f32[64,1,1024]{2,1,0:T(1,128)S(1)}, u32[]{:S(2)}, u32[]{:S(2)}) async-start(f32[64,1,1024]{2,1,0:T(1,128)} %get-tuple-element.20.back_ref), calls=%async_computation.4 | async-start | bytes 524288 | tf_op jit(solution)/shard_map/all_to_all | solution.py:131
  143.0 0.0 copy-start.1
  143.0 0.6 copy-done.1
  143.7 0.0 copy-start
  143.7 5.1 %goal.1 = f32[18,512]{1,0:T(8,128)} custom-call(f32[64,8,512]{2,1,0:T(8,128)S(1)} %all-to-all-done.q_ref, s32[64,8,512]{2,1,0:T(8,128)S(1)} %all-to-all-done.5.ids_ref, f32[64,1,1024]{2,1,0:T(1,128)} %get-tuple-element.20.back_ref, f32[1,128]{1,0:T(1,128)S(1)} %copy-done.1), custom_call_target="tpu_custom_call" | custom-call | flops 20000000 | bytes 2000000 | tf_op jit(solution)/shard_map/goal/pallas_call | solution.py:164
  148.7 6.0 %all-to-all-done.4.back_ref = f32[64,1,1024]{2,1,0:T(1,128)S(1)} async-done(((f32[64,1,1024]{2,1,0:T(1,128)}), f32[64,1,1024]{2,1,0:T(1,128)S(1)}, u32[]{:S(2)}, u32[]{:S(2)}) %all-to-all-start.4) | async-done | bytes 262176 | tf_op jit(solution)/shard_map/all_to_all | solution.py:131
  154.7 0.0 copy-done
  154.7 3.1 %weights.1 = f32[8,32768]{1,0:T(8,128)} custom-call(f32[1,128]{1,0:T(1,128)S(1)} %copy-done.1, f32[8,32768]{1,0:T(8,128)S(1)} %copy-done, f32[64,1,1024]{2,1,0:T(1,128)S(1)} %all-to-all-done.4.back_ref), custom_call_target="tpu_custom_call" | custom-call | flops 1000000 | bytes 2000000 | tf_op jit(solution)/shard_map/weights/pallas_call | solution.py:169
Async XLA Ops:
  0.6 39.5 %all-to-all-start = ((f32[64,8,512]{2,1,0:T(8,128)}), f32[64,8,512]{2,1,0:T(8,128)S(1)}, u32[]{:S(2)}, u32[]{:S(2)}) async-start(f32[64,8,512]{2,1,0:T(8,128)} %bitcast.8), calls=%async_computation | async-start | bytes 2097152 | tf_op jit(solution)/shard_map/all_to_all | solution.py:131
  41.6 22.4 %all-to-all-start.1 = ((f32[256,1,128]{2,1,0:T(1,128)}), f32[256,1,128]{2,1,0:T(1,128)S(1)}, u32[]{:S(2)}, u32[]{:S(2)}) async-start(f32[256,1,128]{2,1,0:T(1,128)} %get-tuple-element.14), calls=%async_computation.1 | async-start | bytes 262144 | tf_op jit(solution)/shard_map/all_to_all | solution.py:131
  103.2 32.9 %all-to-all-start.5 = ((s32[64,8,512]{2,1,0:T(8,128)}), s32[64,8,512]{2,1,0:T(8,128)S(1)}, u32[]{:S(2)}, u32[]{:S(2)}) async-start(s32[64,8,512]{2,1,0:T(8,128)} %bitcast.3), calls=%async_computation.5 | async-start | bytes 2097152 | tf_op jit(solution)/shard_map/all_to_all | solution.py:131
  136.1 18.6 %all-to-all-start.4 = ((f32[64,1,1024]{2,1,0:T(1,128)}), f32[64,1,1024]{2,1,0:T(1,128)S(1)}, u32[]{:S(2)}, u32[]{:S(2)}) async-start(f32[64,1,1024]{2,1,0:T(1,128)} %get-tuple-element.20.back_ref), calls=%async_computation.4 | async-start | bytes 524288 | tf_op jit(solution)/shard_map/all_to_all | solution.py:131
  143.0 0.7 copy-start.1
  143.7 11.1 %copy-start = (f32[8,32768]{1,0:T(8,128)S(1)}, f32[8,32768]{1,0:T(8,128)}, u32[]{:S(2)}) copy-start(f32[8,32768]{1,0:T(8,128)} %x_ref.1) | copy-start | bytes 3145732

commit v2 on v1

--- a/solution.py
+++ b/solution.py
@@ -4,18 +4,20 @@
 from jax import lax
 from jax.experimental import pallas as pl
 from jax.experimental.pallas import tpu as pltpu
+from jax.sharding import Mesh
 from jax.sharding import PartitionSpec as P
 
 NACT = 18
 ITERS = 3
 LANES = 128
-ALL = ("rep", "act")
+ACT = ("x", "z", "core")
+ALL = ("rep", "x", "z", "core")
 VMEM = pl.BlockSpec(memory_space=pltpu.VMEM)
 SMEM = pl.BlockSpec(memory_space=pltpu.SMEM)
 PARAMS = pltpu.CompilerParams(vmem_limit_bytes=8 * 1024 * 1024)
 
 
-def call(body, out_shape, name, n_smem, n_vmem, flops=1_000_000):
+def call(body, out_shape, n_smem, n_vmem, flops=1_000_000):
     n_out = len(out_shape) if isinstance(out_shape, (tuple, list)) else None
     return pl.pallas_call(
         body,
@@ -24,7 +26,6 @@
         out_specs=VMEM if n_out is None else [VMEM] * n_out,
         compiler_params=PARAMS,
         cost_estimate=pl.CostEstimate(flops=flops, bytes_accessed=2_000_000, transcendentals=262_144),
-        name=name,
     )
 
 
@@ -64,24 +65,25 @@
     return jnp.full((1, LANES), scalar, jnp.float32)
 
 
-def first_body(samples, eta_ref, q_ref, top_ref, eta_out, part_ref):
+def first_body(samples, eta_ref, eps_ref, q_ref, top_ref, eta_out, eps_out, part_ref):
     top8 = q_ref[0]
     top8 = lax.fori_loop(1, q_ref.shape[0], lambda i, m: jnp.maximum(m, q_ref[i]), top8)
     top = jnp.max(top8, axis=0, keepdims=True)
     top_ref[...] = top
     eta = row(eta_ref[0])
     eta_out[...] = eta
+    eps_out[...] = row(eps_ref[0])
     part_ref[...] = jnp.broadcast_to(partial_sums(q_ref, top, eta, samples)[None], part_ref.shape)
 
 
 def step_body(samples, states, eps_ref, q_ref, top_ref, eta_ref, gathered_ref, eta_out, part_ref):
-    eta = next_eta(gathered_ref, eta_ref[...], row(eps_ref[0]), states)
+    eta = next_eta(gathered_ref, eta_ref[...], eps_ref[...], states)
     eta_out[...] = eta
     part_ref[...] = jnp.broadcast_to(partial_sums(q_ref, top_ref[...], eta, samples)[None], part_ref.shape)
 
 
 def last_body(samples, states, eps_ref, q_ref, top_ref, eta_ref, gathered_ref, eta_out, back_ref):
-    eta = next_eta(gathered_ref, eta_ref[...], row(eps_ref[0]), states)
+    eta = next_eta(gathered_ref, eta_ref[...], eps_ref[...], states)
     eta_out[...] = eta
     blocks, rows, width = q_ref.shape
     inverse = jnp.broadcast_to((1.0 / eta)[:, :1], (rows, width))
@@ -96,27 +98,56 @@
     back_ref[:, :, width:] = jnp.broadcast_to(scale[None], (copies, 1, width))
 
 
-def goal_body(samples, q_ref, ids_ref, back_ref, eta_ref, goal_ref):
-    blocks, rows, width = q_ref.shape
+def split_body(at_ref, ids_ref, from_core_ref, *out_refs):
+    z, core = at_ref[1], at_ref[2]
+    hops = len(out_refs)
+    for k, out_ref in enumerate(out_refs):
+        to = lax.rem(z + k, hops)
+        for x in range(out_ref.shape[1]):
+            out_ref[0, x] = ids_ref[x, to, core]
+            out_ref[1, x] = from_core_ref[x, to]
+
+
+def merge_body(at_ref, _, *refs):
+    hops = len(refs) * 2 // 3
+    in_refs, out_refs = refs[:hops], refs[hops:]
+    for j, out_ref in enumerate(out_refs):
+        to = lax.rem(at_ref[0] + j, len(out_refs))
+        for k, in_ref in enumerate(in_refs):
+            out_ref[k] = in_ref[:, to]
+
+
+def goal_body(samples, at_ref, q_ref, back_ref, eta_ref, *refs):
+    ids_refs, goal_ref = refs[:-1], refs[-1]
+    across, along, cores = len(ids_refs), ids_refs[0].shape[0], ids_refs[0].shape[1]
+    _, rows, width = q_ref.shape
     inverse = jnp.broadcast_to((1.0 / eta_ref[...])[:, :1], (rows, LANES))
+    x, z, core = at_ref[0], at_ref[1], at_ref[2]
     for tile in range(width // LANES):
         at = slice(tile * LANES, (tile + 1) * LANES)
         top_rows = jnp.broadcast_to(back_ref[0, :, at], (rows, LANES))
         scale = back_ref[0, :, width + tile * LANES : width + (tile + 1) * LANES] * jnp.float32(1.0 / samples)
-
-        def step(i, sums):
-            expo = jnp.exp((q_ref[i, :, at] - top_rows) * inverse)
-            ids = ids_ref[i, :, at]
-            return tuple(s + jnp.where(ids == k, expo, 0.0) for k, s in enumerate(sums))
-
-        zero = jnp.zeros((rows, LANES), jnp.float32)
-        sums = lax.fori_loop(0, blocks, step, (zero,) * NACT, unroll=2)
-        for k, s in enumerate(sums):
-            goal_ref[k : k + 1, at] = jnp.sum(s, axis=0, keepdims=True) * scale
+        sums = (jnp.zeros((rows, LANES), jnp.float32),) * NACT
+        for j, ids_ref in enumerate(ids_refs):
+            from_x = lax.rem(x + across - j, across)
+
+            def step(k, sums):
+                from_z = lax.rem(z + along - k, along)
+                for c in range(cores):
+                    from_core = core if c == 0 else 1 - core
+                    holder = (from_x * along + from_z) * cores + from_core
+                    expo = jnp.exp((q_ref[holder, :, at] - top_rows) * inverse)
+                    ids = ids_ref[k, c, :, at]
+                    sums = tuple(s + jnp.where(ids == n, expo, 0.0) for n, s in enumerate(sums))
+                return sums
+
+            sums = lax.fori_loop(0, along, step, sums)
+        for n, s in enumerate(sums):
+            goal_ref[n : n + 1, at] = jnp.sum(s, axis=0, keepdims=True) * scale
 
 
 def weights_body(eta_ref, x_ref, back_ref, out_ref):
-    rows, width = x_ref.shape
+    rows, _ = x_ref.shape
     owners, _, both = back_ref.shape
     own = both // 2
     inverse = jnp.broadcast_to((1.0 / eta_ref[...])[:, :1], (rows, own))
@@ -131,39 +162,58 @@
     return lax.all_to_all(blocks, axis, split_axis=0, concat_axis=0, tiled=True)
 
 
+def shifted_by(v, axis, hops):
+    size = lax.axis_size(axis)
+    return lax.ppermute(v, axis, [(i, (i + hops) % size) for i in range(size)])
+
+
 def on_device(estimated_returns, chosen_move_ids, previous_eta, trust_region_epsilon):
-    peers = lax.axis_size("act")
+    across, along, cores = (lax.axis_size(a) for a in ACT)
+    peers = lax.axis_size(ACT)
     everyone = peers * lax.axis_size("rep")
     rows, width = estimated_returns.shape
     own = width // peers
     samples, states = rows * peers, width * lax.axis_size("rep")
-    f32 = jnp.float32
+    f32, i32 = jnp.float32, jnp.int32
     shape = jax.ShapeDtypeStruct
-
-    def to_owner(v):
-        return send(v.reshape(rows, peers, own).transpose(1, 0, 2), "act")
-
-    q = to_owner(estimated_returns)
-    ids = to_owner(chosen_move_ids)
-
-    eta_shape, part_shape = shape((1, LANES), f32), shape((everyone, 1, LANES), f32)
-    top, eta, part = call(
-        functools.partial(first_body, samples), [shape((1, own), f32), eta_shape, part_shape], "first", 1, 1
-    )(previous_eta, q)
-    for _ in range(ITERS - 1):
+    at = jnp.stack([lax.axis_index(a) for a in ACT])
+
+    def by_owner(v):
+        return v.reshape(rows, peers, own).transpose(1, 0, 2)
+
+    q = send(by_owner(estimated_returns), ACT)
+
+    moves = by_owner(chosen_move_ids).reshape(across, along, cores, rows, own)
+    give = lax.dynamic_index_in_dim(moves, 1 - at[2], 2, keepdims=False)
+    from_core = shifted_by(give, "core", 1)
+    chunks = call(split_body, [shape((cores, across, rows, own), i32)] * along, 1, 2)(at, moves, from_core)
+    arrived = [chunks[0]]
+    for k in range(1, along):
+        arrived.append(shifted_by(chunks[k], "z", k))
+
+    row_shape, part_shape = shape((1, LANES), f32), shape((everyone, 1, LANES), f32)
+    top, eta, eps, part = call(
+        functools.partial(first_body, samples), [shape((1, own), f32), row_shape, row_shape, part_shape], 2, 1
+    )(previous_eta, trust_region_epsilon, q)
+    for i in range(ITERS - 1):
         gathered = send(part, ALL)
         eta, part = call(
-            functools.partial(step_body, samples, states), [eta_shape, part_shape], "step", 1, 4
-        )(trust_region_epsilon, q, top, eta, gathered)
+            functools.partial(step_body, samples, states), [row_shape, part_shape], 0, 5
+        )(eps, q, top, eta, gathered)
+        if i == 1:
+            chunks = call(merge_body, [shape((along, cores, rows, own), i32)] * across, 1, 1 + along)(at, eta, *arrived)
+            ids = [chunks[0]]
+            for j in range(1, across):
+                ids.append(shifted_by(chunks[j], "x", j))
     gathered = send(part, ALL)
     eta, back = call(
         functools.partial(last_body, samples, states),
-        [eta_shape, shape((peers, 1, 2 * own), f32)], "last", 1, 4,
-    )(trust_region_epsilon, q, top, eta, gathered)
-    everywhere = send(back, "act")
+        [row_shape, shape((peers, 1, 2 * own), f32)], 0, 5,
+    )(eps, q, top, eta, gathered)
+    everywhere = send(back, ACT)
     goal = call(
-        functools.partial(goal_body, samples), shape((NACT, own), f32), "goal", 0, 4, flops=20_000_000
-    )(q, ids, back, eta)
+        functools.partial(goal_body, samples), shape((NACT, own), f32), 1, 3 + across, flops=20_000_000
+    )(at, q, back, eta, *ids)
 
     steps = 8
     weights = pl.pallas_call(
@@ -184,11 +234,12 @@
 
 
 def solution(mesh):
-    placed = (P("act", "rep"), P("act", "rep"), P(), P())
+    split = Mesh(mesh.devices.reshape(4, 8, 2, mesh.shape["rep"]), (*ACT, "rep"))
+    placed = (P(ACT, "rep"), P(ACT, "rep"), P(), P())
     return jax.shard_map(
         on_device,
-        mesh=mesh,
+        mesh=split,
         in_specs=placed,
-        out_specs=(P("act", "rep"), P(None, ALL), P()),
+        out_specs=(P(ACT, "rep"), P(None, ALL), P()),
         check_vma=False,
     )

time: 160 us -> 170 us (1.062); the launches traced: 158 us -> 170 us
  starting transfers between devices: 33.1 us -> 55.3 us
  blocking collectives: 37.2 us -> 18.6 us
  waiting for transfers between devices: 71.8 us -> 76.9 us
  Pallas kernels: 13.1 us -> 16 us
    ppermute x0 -> x11, waiting for transfers between devices: none -> 32.6 us  [shifted_by(): return lax.ppermute(v, axis, [(i, (i + hops) % size) for i in range(size)])]
    all_to_all x4, waiting for transfers between devices: 71.8 us -> 44.4 us  [send(): return lax.all_to_all(blocks, axis, split_axis=0, concat_axis=0, tiled=True)]
    ppermute x0 -> x11, starting transfers between devices: none -> 23 us  [shifted_by(): return lax.ppermute(v, axis, [(i, (i + hops) % size) for i in range(size)])]
    all_to_all x2 -> x1, blocking collectives: 37.2 us -> 18.6 us  [send(): return lax.all_to_all(blocks, axis, split_axis=0, concat_axis=0, tiled=True)]
    pallas_call x5 -> x7, Pallas kernels: 9.98 us -> 12.8 us  [the longest x1 5.33 us: on_device(): call(functools.partial(goal_body, samples), shape((NACT, own), f32), 1, 3...]
  transfers between devices with their start and end apart: 4 -> 15, of which waited for: 4 -> 9; matrix products, arithmetic and copies ran while one was open for 0% -> 0% of each run, Pallas kernels for 4% -> 7%
where the time goes in v2:
time: 170 us
  waiting for transfers between devices  76.9 us (45%)
  starting transfers between devices  55.3 us (33%)
  blocking collectives  18.6 us (11%)
  Pallas kernels  16 us (9%)
  between operations  2.11 us (1%)
    all_to_all x4, waiting for transfers between devices, send(): return lax.all_to_all(blocks, axis, split_axis=0, concat_axis=0, tiled=True)  44.4 us
    ppermute x11, waiting for transfers between devices, shifted_by(): return lax.ppermute(v, axis, [(i, (i + hops) % size) for i in range(size)])  32.6 us
    all_to_all x4, starting transfers between devices, send(): return lax.all_to_all(blocks, axis, split_axis=0, concat_axis=0, tiled=True)  32.3 us
    ppermute x11, starting transfers between devices, shifted_by(): return lax.ppermute(v, axis, [(i, (i + hops) % size) for i in range(size)])  23 us
    all_to_all x1, blocking collectives, send(): return lax.all_to_all(blocks, axis, split_axis=0, concat_axis=0, tiled=True)  18.6 us
    pallas_call x1, Pallas kernels, on_device(): call(functools.partial(goal_body, samples), shape((NACT, own), f32), 1, 3...  5.33 us
  transfers between devices with their start and end apart: 15, of which 9 were waited for; matrix products, arithmetic and copies ran while one was open for 0% of the time, Pallas kernels for 7%

profile of v2, /device:TPU:32, one launch (start us, length us, event | category | flops | bytes accessed | tf_op | source)
XLA Modules:
  0.0 169.7 jit_solution(14956304084194508032)
XLA Ops:
  0.6 11.6 %all-to-all-start = ((f32[64,8,512]{2,1,0:T(8,128)}), f32[64,8,512]{2,1,0:T(8,128)S(1)}, u32[]{:S(2)}, u32[]{:S(2)}) async-start(f32[64,8,512]{2,1,0:T(8,128)} %bitcast.15), calls=%async_computation | async-start | bytes 2097152 | tf_op jit(solution)/shard_map/all_to_all | solution.py:162
  13.6 26.5 %all-to-all-done.q_ref = f32[64,8,512]{2,1,0:T(8,128)S(1)} async-done(((f32[64,8,512]{2,1,0:T(8,128)}), f32[64,8,512]{2,1,0:T(8,128)S(1)}, u32[]{:S(2)}, u32[]{:S(2)}) %all-to-all-start) | async-done | bytes 1048608 | tf_op jit(solution)/shard_map/all_to_all | solution.py:162
  41.6 9.7 %all-to-all-start.1 = ((f32[256,1,128]{2,1,0:T(1,128)}), f32[256,1,128]{2,1,0:T(1,128)S(1)}, u32[]{:S(2)}, u32[]{:S(2)}) async-start(f32[256,1,128]{2,1,0:T(1,128)} %get-tuple-element.28), calls=%async_computation.1 | async-start | bytes 262144 | tf_op jit(solution)/shard_map/all_to_all | solution.py:162
  51.6 12.4 %all-to-all-done.1.gathered_ref = f32[256,1,128]{2,1,0:T(1,128)S(1)} async-done(((f32[256,1,128]{2,1,0:T(1,128)}), f32[256,1,128]{2,1,0:T(1,128)S(1)}, u32[]{:S(2)}, u32[]{:S(2)}) %all-to-all-start.1) | async-done | bytes 131104 | tf_op jit(solution)/shard_map/all_to_all | solution.py:162
  65.0 18.6 %all_to_all.25.gathered_ref = f32[256,1,128]{2,1,0:T(1,128)S(1)} all-to-all(f32[256,1,128]{2,1,0:T(1,128)S(1)} %get-tuple-element.30), channel_id=1, replica_groups=mesh['x'=4,'z'=8,'core'=2,'rep'=4] {'rep','x','z','core'}, dimensions={0} | all-to-all | bytes 262144 | tf_op jit(solution)/shard_map/all_to_all | solution.py:162
  83.6 1.6 shard_map.69
  85.2 6.1 %all-to-all-start.3 = ((f32[256,1,128]{2,1,0:T(1,128)}), f32[256,1,128]{2,1,0:T(1,128)S(1)}, u32[]{:S(2)}, u32[]{:S(2)}) async-start(f32[256,1,128]{2,1,0:T(1,128)} %get-tuple-element.32), calls=%async_computation.3 | async-start | bytes 262144 | tf_op jit(solution)/shard_map/all_to_all | solution.py:162
  92.8 1.7 %collective-permute-start.1 = (s32[2,4,8,512]{3,2,1,0:T(8,128)}, s32[2,4,8,512]{3,2,1,0:T(8,128)S(1)}, u32[]{:S(2)}, u32[]{:S(2)}) collective-permute-start(s32[2,4,8,512]{3,2,1,0:T(8,128)} %get-tuple-element.36), channel_id=1, source_target_pairs={{0,8},{8,16},{16,24},{24,32},{32,40},{40,48},{48,56},{56,0},{1,9},... | collective-permute-start | bytes 393224 | tf_op jit(solution)/shard_map/ppermute | solution.py:167
  94.5 4.1 %collective-permute-start.2 = (s32[2,4,8,512]{3,2,1,0:T(8,128)}, s32[2,4,8,512]{3,2,1,0:T(8,128)S(1)}, u32[]{:S(2)}, u32[]{:S(2)}) collective-permute-start(s32[2,4,8,512]{3,2,1,0:T(8,128)} %get-tuple-element.37), channel_id=1, source_target_pairs={{0,16},{8,24},{16,32},{24,40},{32,48},{40,56},{48,0},{56,8},{1,17}... | collective-permute-start | bytes 393224 | tf_op jit(solution)/shard_map/ppermute | solution.py:167
  98.6 5.5 %all-to-all-done.3.gathered_ref = f32[256,1,128]{2,1,0:T(1,128)S(1)} async-done(((f32[256,1,128]{2,1,0:T(1,128)}), f32[256,1,128]{2,1,0:T(1,128)S(1)}, u32[]{:S(2)}, u32[]{:S(2)}) %all-to-all-start.3) | async-done | bytes 131104 | tf_op jit(solution)/shard_map/all_to_all | solution.py:162
  105.5 4.9 %all-to-all-start.4 = ((f32[64,1,1024]{2,1,0:T(1,128)}), f32[64,1,1024]{2,1,0:T(1,128)S(1)}, u32[]{:S(2)}, u32[]{:S(2)}) async-start(f32[64,1,1024]{2,1,0:T(1,128)} %get-tuple-element.34.back_ref), calls=%async_computation.4 | async-start | bytes 524288 | tf_op jit(solution)/shard_map/all_to_all | solution.py:162
  110.5 4.6 %collective-permute-start.3 = (s32[2,4,8,512]{3,2,1,0:T(8,128)S(1)}, s32[2,4,8,512]{3,2,1,0:T(8,128)S(1)}, u32[]{:S(2)}, u32[]{:S(2)}) collective-permute-start(s32[2,4,8,512]{3,2,1,0:T(8,128)S(1)} %get-tuple-element.38), channel_id=1, source_target_pairs={{0,24},{8,32},{16,40},{24,48},{32,56},{40,0},{48,8},{56,16},{1,25}... | collective-permute-start | bytes 393224 | tf_op jit(solution)/shard_map/ppermute | solution.py:167
  115.6 4.5 %collective-permute-start.5 = (s32[2,4,8,512]{3,2,1,0:T(8,128)S(1)}, s32[2,4,8,512]{3,2,1,0:T(8,128)S(1)}, u32[]{:S(2)}, u32[]{:S(2)}) collective-permute-start(s32[2,4,8,512]{3,2,1,0:T(8,128)S(1)} %get-tuple-element.40), channel_id=1, source_target_pairs={{0,40},{8,48},{16,56},{24,0},{32,8},{40,16},{48,24},{56,32},{1,41}... | collective-permute-start | bytes 393224 | tf_op jit(solution)/shard_map/ppermute | solution.py:167
  120.3 1.8 %collective-permute-start.7 = (s32[2,4,8,512]{3,2,1,0:T(8,128)S(1)}, s32[2,4,8,512]{3,2,1,0:T(8,128)S(1)}, u32[]{:S(2)}, u32[]{:S(2)}) collective-permute-start(s32[2,4,8,512]{3,2,1,0:T(8,128)S(1)} %get-tuple-element.42), channel_id=1, source_target_pairs={{0,56},{8,0},{16,8},{24,16},{32,24},{40,32},{48,40},{56,48},{1,57}... | collective-permute-start | bytes 393224 | tf_op jit(solution)/shard_map/ppermute | solution.py:167
  122.1 3.3 %collective-permute-done.3.refs_3_ = s32[2,4,8,512]{3,2,1,0:T(8,128)S(1)} collective-permute-done((s32[2,4,8,512]{3,2,1,0:T(8,128)S(1)}, s32[2,4,8,512]{3,2,1,0:T(8,128)S(1)}, u32[]{:S(2)}, u32[]{:S(2)}) %collective-permute-start.3) | collective-permute-done | bytes 131104 | tf_op jit(solution)/shard_map/ppermute | solution.py:167
  125.4 4.0 %collective-permute-done.4.refs_4_ = s32[2,4,8,512]{3,2,1,0:T(8,128)S(1)} collective-permute-done((s32[2,4,8,512]{3,2,1,0:T(8,128)S(1)}, s32[2,4,8,512]{3,2,1,0:T(8,128)S(1)}, u32[]{:S(2)}, u32[]{:S(2)}) %collective-permute-start.4) | collective-permute-done | bytes 131104 | tf_op jit(solution)/shard_map/ppermute | solution.py:167
  129.4 8.7 %collective-permute-done.5.refs_5_ = s32[2,4,8,512]{3,2,1,0:T(8,128)S(1)} collective-permute-done((s32[2,4,8,512]{3,2,1,0:T(8,128)S(1)}, s32[2,4,8,512]{3,2,1,0:T(8,128)S(1)}, u32[]{:S(2)}, u32[]{:S(2)}) %collective-permute-start.5) | collective-permute-done | bytes 131104 | tf_op jit(solution)/shard_map/ppermute | solution.py:167
  138.1 4.0 %collective-permute-done.7.refs_7_ = s32[2,4,8,512]{3,2,1,0:T(8,128)S(1)} collective-permute-done((s32[2,4,8,512]{3,2,1,0:T(8,128)S(1)}, s32[2,4,8,512]{3,2,1,0:T(8,128)S(1)}, u32[]{:S(2)}, u32[]{:S(2)}) %collective-permute-start.7) | collective-permute-done | bytes 131104 | tf_op jit(solution)/shard_map/ppermute | solution.py:167
  142.7 3.1 %collective-permute-start.10 = (s32[8,2,8,512]{3,2,1,0:T(8,128)S(1)}, s32[8,2,8,512]{3,2,1,0:T(8,128)S(1)}, u32[]{:S(2)}, u32[]{:S(2)}) collective-permute-start(s32[8,2,8,512]{3,2,1,0:T(8,128)S(1)} %get-tuple-element.46), channel_id=1, source_target_pairs={{0,192},{64,0},{128,64},{192,128},{1,193},{65,1},{129,65},{193,129... | collective-permute-start | bytes 786440 | tf_op jit(solution)/shard_map/ppermute | solution.py:167
  145.8 2.2 %collective-permute-start.9 = (s32[8,2,8,512]{3,2,1,0:T(8,128)S(1)}, s32[8,2,8,512]{3,2,1,0:T(8,128)S(1)}, u32[]{:S(2)}, u32[]{:S(2)}) collective-permute-start(s32[8,2,8,512]{3,2,1,0:T(8,128)S(1)} %get-tuple-element.45), channel_id=1, source_target_pairs={{0,128},{64,192},{128,0},{192,64},{1,129},{65,193},{129,1},{193,65... | collective-permute-start | bytes 786440 | tf_op jit(solution)/shard_map/ppermute | solution.py:167
  148.0 9.1 %collective-permute-done.10.refs_3_ = s32[8,2,8,512]{3,2,1,0:T(8,128)S(1)} collective-permute-done((s32[8,2,8,512]{3,2,1,0:T(8,128)S(1)}, s32[8,2,8,512]{3,2,1,0:T(8,128)S(1)}, u32[]{:S(2)}, u32[]{:S(2)}) %collective-permute-start.10) | collective-permute-done | bytes 262176 | tf_op jit(solution)/shard_map/ppermute | solution.py:167
  157.2 3.4 %collective-permute-done.8.refs_1_ = s32[8,2,8,512]{3,2,1,0:T(8,128)S(1)} collective-permute-done((s32[8,2,8,512]{3,2,1,0:T(8,128)S(1)}, s32[8,2,8,512]{3,2,1,0:T(8,128)S(1)}, u32[]{:S(2)}, u32[]{:S(2)}) %collective-permute-start.8) | collective-permute-done | bytes 262176 | tf_op jit(solution)/shard_map/ppermute | solution.py:167
  161.2 5.3 %shard_map.73 = f32[18,512]{1,0:T(8,128)} custom-call(s32[3]{0:T(128)S(1)} %pad_add_fusion.at_ref, f32[64,8,512]{2,1,0:T(8,128)S(1)} %all-to-all-done.q_ref, f32[64,1,1024]{2,1,0:T(1,128)} %get-tuple-element.34.back_ref, f32[1,128]{1,0:T(1,128)S(1)} %copy-done.2, s32[8,2,8,512]{3,2,1,0:T(8,128)S(1)} %get-tuple-element.43.refs_0_, ...), custom_call_target="tpu_custom_call" | custom-call | flops 20000000 | bytes 2000000 | tf_op jit(solution)/shard_map/pallas_call | solution.py:214
  166.6 3.1 %weights.1 = f32[8,32768]{1,0:T(8,128)} custom-call(f32[1,128]{1,0:T(1,128)S(1)} %copy-done.2, f32[8,32768]{1,0:T(8,128)S(1)} %copy-done, f32[64,1,1024]{2,1,0:T(1,128)S(1)} %all-to-all-done.4.back_ref), custom_call_target="tpu_custom_call" | custom-call | flops 1000000 | bytes 2000000 | tf_op jit(solution)/shard_map/weights/pallas_call | solution.py:219
  (23 shorter events, 7.6 us)
Async XLA Ops:
  0.6 39.5 %all-to-all-start = ((f32[64,8,512]{2,1,0:T(8,128)}), f32[64,8,512]{2,1,0:T(8,128)S(1)}, u32[]{:S(2)}, u32[]{:S(2)}) async-start(f32[64,8,512]{2,1,0:T(8,128)} %bitcast.15), calls=%async_computation | async-start | bytes 2097152 | tf_op jit(solution)/shard_map/all_to_all | solution.py:162
  12.2 39.1 %copy-start.1 = (s32[8,32768]{1,0:T(8,128)S(1)}, s32[8,32768]{1,0:T(8,128)}, u32[]{:S(2)}) copy-start(s32[8,32768]{1,0:T(8,128)} %param.5) | copy-start | bytes 3145732
  41.6 22.4 %all-to-all-start.1 = ((f32[256,1,128]{2,1,0:T(1,128)}), f32[256,1,128]{2,1,0:T(1,128)S(1)}, u32[]{:S(2)}, u32[]{:S(2)}) async-start(f32[256,1,128]{2,1,0:T(1,128)} %get-tuple-element.28), calls=%async_computation.1 | async-start | bytes 262144 | tf_op jit(solution)/shard_map/all_to_all | solution.py:162
  51.4 40.1 %collective-permute-start = (s32[4,8,8,512]{3,2,1,0:T(8,128)S(1)}, s32[4,8,8,512]{3,2,1,0:T(8,128)S(1)}, u32[]{:S(2)}, u32[]{:S(2)}) collective-permute-start(s32[4,8,8,512]{3,2,1,0:T(8,128)S(1)} %dynamic-slice_bitcast_fusion), channel_id=1, source_target_pairs={{0,4},{4,0},{1,5},{5,1},{2,6},{6,2},{3,7},{7,3},{8,12},{12,8},{9,1... | collective-permute-start | bytes 1572872 | tf_op jit(solution)/shard_map/ppermute | solution.py:167
  85.2 18.8 %all-to-all-start.3 = ((f32[256,1,128]{2,1,0:T(1,128)}), f32[256,1,128]{2,1,0:T(1,128)S(1)}, u32[]{:S(2)}, u32[]{:S(2)}) async-start(f32[256,1,128]{2,1,0:T(1,128)} %get-tuple-element.32), calls=%async_computation.3 | async-start | bytes 262144 | tf_op jit(solution)/shard_map/all_to_all | solution.py:162
  92.8 27.3 %collective-permute-start.1 = (s32[2,4,8,512]{3,2,1,0:T(8,128)}, s32[2,4,8,512]{3,2,1,0:T(8,128)S(1)}, u32[]{:S(2)}, u32[]{:S(2)}) collective-permute-start(s32[2,4,8,512]{3,2,1,0:T(8,128)} %get-tuple-element.36), channel_id=1, source_target_pairs={{0,8},{8,16},{16,24},{24,32},{32,40},{40,48},{48,56},{56,0},{1,9},... | collective-permute-start | bytes 393224 | tf_op jit(solution)/shard_map/ppermute | solution.py:167
  94.5 25.8 %collective-permute-start.2 = (s32[2,4,8,512]{3,2,1,0:T(8,128)}, s32[2,4,8,512]{3,2,1,0:T(8,128)S(1)}, u32[]{:S(2)}, u32[]{:S(2)}) collective-permute-start(s32[2,4,8,512]{3,2,1,0:T(8,128)} %get-tuple-element.37), channel_id=1, source_target_pairs={{0,16},{8,24},{16,32},{24,40},{32,48},{40,56},{48,0},{56,8},{1,17}... | collective-permute-start | bytes 393224 | tf_op jit(solution)/shard_map/ppermute | solution.py:167
  105.5 61.1 %all-to-all-start.4 = ((f32[64,1,1024]{2,1,0:T(1,128)}), f32[64,1,1024]{2,1,0:T(1,128)S(1)}, u32[]{:S(2)}, u32[]{:S(2)}) async-start(f32[64,1,1024]{2,1,0:T(1,128)} %get-tuple-element.34.back_ref), calls=%async_computation.4 | async-start | bytes 524288 | tf_op jit(solution)/shard_map/all_to_all | solution.py:162
  110.5 15.0 %collective-permute-start.3 = (s32[2,4,8,512]{3,2,1,0:T(8,128)S(1)}, s32[2,4,8,512]{3,2,1,0:T(8,128)S(1)}, u32[]{:S(2)}, u32[]{:S(2)}) collective-permute-start(s32[2,4,8,512]{3,2,1,0:T(8,128)S(1)} %get-tuple-element.38), channel_id=1, source_target_pairs={{0,24},{8,32},{16,40},{24,48},{32,56},{40,0},{48,8},{56,16},{1,25}... | collective-permute-start | bytes 393224 | tf_op jit(solution)/shard_map/ppermute | solution.py:167
  115.0 14.4 %collective-permute-start.4 = (s32[2,4,8,512]{3,2,1,0:T(8,128)S(1)}, s32[2,4,8,512]{3,2,1,0:T(8,128)S(1)}, u32[]{:S(2)}, u32[]{:S(2)}) collective-permute-start(s32[2,4,8,512]{3,2,1,0:T(8,128)S(1)} %get-tuple-element.39), channel_id=1, source_target_pairs={{0,32},{8,40},{16,48},{24,56},{32,0},{40,8},{48,16},{56,24},{1,33}... | collective-permute-start | bytes 393224 | tf_op jit(solution)/shard_map/ppermute | solution.py:167
  115.6 22.6 %collective-permute-start.5 = (s32[2,4,8,512]{3,2,1,0:T(8,128)S(1)}, s32[2,4,8,512]{3,2,1,0:T(8,128)S(1)}, u32[]{:S(2)}, u32[]{:S(2)}) collective-permute-start(s32[2,4,8,512]{3,2,1,0:T(8,128)S(1)} %get-tuple-element.40), channel_id=1, source_target_pairs={{0,40},{8,48},{16,56},{24,0},{32,8},{40,16},{48,24},{56,32},{1,41}... | collective-permute-start | bytes 393224 | tf_op jit(solution)/shard_map/ppermute | solution.py:167
  120.1 18.0 %collective-permute-start.6 = (s32[2,4,8,512]{3,2,1,0:T(8,128)S(1)}, s32[2,4,8,512]{3,2,1,0:T(8,128)S(1)}, u32[]{:S(2)}, u32[]{:S(2)}) collective-permute-start(s32[2,4,8,512]{3,2,1,0:T(8,128)S(1)} %get-tuple-element.41), channel_id=1, source_target_pairs={{0,48},{8,56},{16,0},{24,8},{32,16},{40,24},{48,32},{56,40},{1,49}... | collective-permute-start | bytes 393224 | tf_op jit(solution)/shard_map/ppermute | solution.py:167
  120.3 21.8 %collective-permute-start.7 = (s32[2,4,8,512]{3,2,1,0:T(8,128)S(1)}, s32[2,4,8,512]{3,2,1,0:T(8,128)S(1)}, u32[]{:S(2)}, u32[]{:S(2)}) collective-permute-start(s32[2,4,8,512]{3,2,1,0:T(8,128)S(1)} %get-tuple-element.42), channel_id=1, source_target_pairs={{0,56},{8,0},{16,8},{24,16},{32,24},{40,32},{48,40},{56,48},{1,57}... | collective-permute-start | bytes 393224 | tf_op jit(solution)/shard_map/ppermute | solution.py:167
  142.7 14.4 %collective-permute-start.10 = (s32[8,2,8,512]{3,2,1,0:T(8,128)S(1)}, s32[8,2,8,512]{3,2,1,0:T(8,128)S(1)}, u32[]{:S(2)}, u32[]{:S(2)}) collective-permute-start(s32[8,2,8,512]{3,2,1,0:T(8,128)S(1)} %get-tuple-element.46), channel_id=1, source_target_pairs={{0,192},{64,0},{128,64},{192,128},{1,193},{65,1},{129,65},{193,129... | collective-permute-start | bytes 786440 | tf_op jit(solution)/shard_map/ppermute | solution.py:167
  145.8 14.8 %collective-permute-start.8 = (s32[8,2,8,512]{3,2,1,0:T(8,128)S(1)}, s32[8,2,8,512]{3,2,1,0:T(8,128)S(1)}, u32[]{:S(2)}, u32[]{:S(2)}) collective-permute-start(s32[8,2,8,512]{3,2,1,0:T(8,128)S(1)} %get-tuple-element.44), channel_id=1, source_target_pairs={{0,64},{64,128},{128,192},{192,0},{1,65},{65,129},{129,193},{193,1... | collective-permute-start | bytes 786440 | tf_op jit(solution)/shard_map/ppermute | solution.py:167
  145.8 14.8 %collective-permute-start.9 = (s32[8,2,8,512]{3,2,1,0:T(8,128)S(1)}, s32[8,2,8,512]{3,2,1,0:T(8,128)S(1)}, u32[]{:S(2)}, u32[]{:S(2)}) collective-permute-start(s32[8,2,8,512]{3,2,1,0:T(8,128)S(1)} %get-tuple-element.45), channel_id=1, source_target_pairs={{0,128},{64,192},{128,0},{192,64},{1,129},{65,193},{129,1},{193,65... | collective-permute-start | bytes 786440 | tf_op jit(solution)/shard_map/ppermute | solution.py:167
  160.6 0.7 copy-start.2
  161.2 5.3 %copy-start = (f32[8,32768]{1,0:T(8,128)S(1)}, f32[8,32768]{1,0:T(8,128)}, u32[]{:S(2)}) copy-start(f32[8,32768]{1,0:T(8,128)} %x_ref.1) | copy-start | bytes 3145732

commit v3 on v2

--- a/solution.py
+++ b/solution.py
@@ -12,6 +12,8 @@
 LANES = 128
 ACT = ("x", "z", "core")
 ALL = ("rep", "x", "z", "core")
+CHIPS = ("rep", "x", "z")
+PLANE = ("x", "z")
 VMEM = pl.BlockSpec(memory_space=pltpu.VMEM)
 SMEM = pl.BlockSpec(memory_space=pltpu.SMEM)
 PARAMS = pltpu.CompilerParams(vmem_limit_bytes=8 * 1024 * 1024)
@@ -73,13 +75,13 @@
     eta = row(eta_ref[0])
     eta_out[...] = eta
     eps_out[...] = row(eps_ref[0])
-    part_ref[...] = jnp.broadcast_to(partial_sums(q_ref, top, eta, samples)[None], part_ref.shape)
+    part_ref[...] = partial_sums(q_ref, top, eta, samples)
 
 
 def step_body(samples, states, eps_ref, q_ref, top_ref, eta_ref, gathered_ref, eta_out, part_ref):
     eta = next_eta(gathered_ref, eta_ref[...], eps_ref[...], states)
     eta_out[...] = eta
-    part_ref[...] = jnp.broadcast_to(partial_sums(q_ref, top_ref[...], eta, samples)[None], part_ref.shape)
+    part_ref[...] = partial_sums(q_ref, top_ref[...], eta, samples)
 
 
 def last_body(samples, states, eps_ref, q_ref, top_ref, eta_ref, gathered_ref, eta_out, back_ref):
@@ -146,16 +148,25 @@
             goal_ref[n : n + 1, at] = jnp.sum(s, axis=0, keepdims=True) * scale
 
 
-def weights_body(eta_ref, x_ref, back_ref, out_ref):
-    rows, _ = x_ref.shape
-    owners, _, both = back_ref.shape
+def weights_body(steps, at_ref, eta_ref, x_ref, same_ref, other_ref, out_ref, held, sems):
+    rows, width = x_ref.shape
+    chips, _, both = same_ref.shape
     own = both // 2
     inverse = jnp.broadcast_to((1.0 / eta_ref[...])[:, :1], (rows, own))
-    for j in range(owners):
-        at = slice(j * own, (j + 1) * own)
-        top = jnp.broadcast_to(back_ref[j, :, :own], (rows, own))
-        scale = jnp.broadcast_to(back_ref[j, :, own:], (rows, own))
-        out_ref[:, at] = jnp.exp((x_ref[:, at] - top) * inverse) * scale
+    core = at_ref[2]
+    copies = []
+    for step in range(steps):
+        for chip in range(step * chips // steps, (step + 1) * chips // steps):
+            for from_ref, owner in ((same_ref, chip * 2 + core), (other_ref, chip * 2 + 1 - core)):
+                at = pl.ds(pl.multiple_of(owner * own, own), own)
+                top = jnp.broadcast_to(from_ref[chip, :, :own], (rows, own))
+                scale = jnp.broadcast_to(from_ref[chip, :, own:], (rows, own))
+                held[:, at] = jnp.exp((x_ref[:, at] - top) * inverse) * scale
+        part = pl.ds(step * width // steps, width // steps)
+        copies.append(pltpu.make_async_copy(held.at[:, part], out_ref.at[:, part], sems.at[step]))
+        copies[-1].start()
+    for copy in copies:
+        copy.wait()
 
 
 def send(blocks, axis):
@@ -191,45 +202,47 @@
     for k in range(1, along):
         arrived.append(shifted_by(chunks[k], "z", k))
 
-    row_shape, part_shape = shape((1, LANES), f32), shape((everyone, 1, LANES), f32)
+    row_shape = shape((1, LANES), f32)
+
+    def sums_of_chips(part):
+        chip = part + shifted_by(part, "core", 1)
+        return send(jnp.broadcast_to(chip[None], (everyone // cores, 1, LANES)), CHIPS)
+
     top, eta, eps, part = call(
-        functools.partial(first_body, samples), [shape((1, own), f32), row_shape, row_shape, part_shape], 2, 1
+        functools.partial(first_body, samples), [shape((1, own), f32), row_shape, row_shape, row_shape], 2, 1
     )(previous_eta, trust_region_epsilon, q)
     for i in range(ITERS - 1):
-        gathered = send(part, ALL)
+        gathered = sums_of_chips(part)
         eta, part = call(
-            functools.partial(step_body, samples, states), [row_shape, part_shape], 0, 5
+            functools.partial(step_body, samples, states), [row_shape, row_shape], 0, 5
         )(eps, q, top, eta, gathered)
         if i == 1:
             chunks = call(merge_body, [shape((along, cores, rows, own), i32)] * across, 1, 1 + along)(at, eta, *arrived)
             ids = [chunks[0]]
             for j in range(1, across):
                 ids.append(shifted_by(chunks[j], "x", j))
-    gathered = send(part, ALL)
+    gathered = sums_of_chips(part)
     eta, back = call(
         functools.partial(last_body, samples, states),
-        [row_shape, shape((peers, 1, 2 * own), f32)], 0, 5,
+        [row_shape, shape((peers // cores, 1, 2 * own), f32)], 0, 5,
     )(eps, q, top, eta, gathered)
-    everywhere = send(back, ACT)
+    from_same = send(back, PLANE)
+    from_other = shifted_by(from_same, "core", 1)
     goal = call(
         functools.partial(goal_body, samples), shape((NACT, own), f32), 1, 3 + across, flops=20_000_000
     )(at, q, back, eta, *ids)
 
-    steps = 8
+    steps = 4
     weights = pl.pallas_call(
-        weights_body,
-        grid=(steps,),
+        functools.partial(weights_body, steps),
         out_shape=shape((rows, width), f32),
-        in_specs=[
-            pl.BlockSpec((1, LANES), lambda i: (0, 0)),
-            pl.BlockSpec((rows, width // steps), lambda i: (0, i)),
-            pl.BlockSpec((peers // steps, 1, 2 * own), lambda i: (i, 0, 0)),
-        ],
-        out_specs=pl.BlockSpec((rows, width // steps), lambda i: (0, i)),
+        in_specs=[SMEM] + [VMEM] * 4,
+        out_specs=pl.BlockSpec(memory_space=pl.ANY),
+        scratch_shapes=[pltpu.VMEM((rows, width), f32), pltpu.SemaphoreType.DMA((steps,))],
         compiler_params=PARAMS,
         cost_estimate=pl.CostEstimate(flops=1_000_000, bytes_accessed=2_000_000, transcendentals=262_144),
         name="weights",
-    )(eta, estimated_returns, everywhere)
+    )(at, eta, estimated_returns, from_same, from_other)
     return weights, goal, eta[0, :1]
 
 

time: 170 us -> 151 us (0.89); the launches traced: 170 us -> 148 us
  blocking collectives: 18.6 us -> 0 us
  waiting for transfers between devices: 76.9 us -> 64.3 us
  starting transfers between devices: 55.3 us -> 66.2 us
  Pallas kernels: 16 us -> 12.4 us
  local copies, waits for them, and re-layouts: 0.71 us -> 2.71 us
    all_to_all x1 -> x0, blocking collectives: 18.6 us -> none  [send(): return lax.all_to_all(blocks, axis, split_axis=0, concat_axis=0, tiled=True)]
    ppermute x11 -> x15, waiting for transfers between devices: 32.6 us -> 15.4 us  [shifted_by(): return lax.ppermute(v, axis, [(i, (i + hops) % size) for i in range(size)])]
    all_to_all x4 -> x5, starting transfers between devices: 32.3 us -> 46.7 us  [send(): return lax.all_to_all(blocks, axis, split_axis=0, concat_axis=0, tiled=True)]
    all_to_all x4 -> x5, waiting for transfers between devices: 44.4 us -> 48.9 us  [send(): return lax.all_to_all(blocks, axis, split_axis=0, concat_axis=0, tiled=True)]
    ppermute x11 -> x15, starting transfers between devices: 23 us -> 19.5 us  [shifted_by(): return lax.ppermute(v, axis, [(i, (i + hops) % size) for i in range(size)])]
    pallas_call x3, Pallas kernels: 5.78 us -> 3.24 us  [the longest x1 1.67 us: on_device(): pl.pallas_call(functools.partial(weights_body, steps), out_shape=shape((r...]
    broadcast_in_dim x0 -> x3, local copies, waits for them, and re-layouts: none -> 1.99 us  [sums_of_chips(): jnp.broadcast_to(chip[None], (everyone // cores, 1, LANES))]
  transfers between devices with their start and end apart: 15 -> 20, of which waited for: 9 -> 9; matrix products, arithmetic and copies ran while one was open for 0% -> 1% of each run, Pallas kernels for 7% -> 7%
where the time goes in v3:
time: 151 us; the launch traced here: 148 us
  starting transfers between devices  66.2 us (44%)
  waiting for transfers between devices  64.3 us (43%)
  Pallas kernels  12.4 us (8%)
  local copies, waits for them, and re-layouts  2.71 us (2%)
  between operations  2.31 us (2%)
    all_to_all x5, waiting for transfers between devices, send(): return lax.all_to_all(blocks, axis, split_axis=0, concat_axis=0, tiled=True)  48.9 us
    all_to_all x5, starting transfers between devices, send(): return lax.all_to_all(blocks, axis, split_axis=0, concat_axis=0, tiled=True)  46.7 us
    ppermute x15, starting transfers between devices, shifted_by(): return lax.ppermute(v, axis, [(i, (i + hops) % size) for i in range(size)])  19.5 us
    ppermute x15, waiting for transfers between devices, shifted_by(): return lax.ppermute(v, axis, [(i, (i + hops) % size) for i in range(size)])  15.4 us
    pallas_call x1, Pallas kernels, on_device(): call(functools.partial(goal_body, samples), shape((NACT, own), f32), 1, 3...  5.28 us
  transfers between devices with their start and end apart: 20, of which 9 were waited for; matrix products, arithmetic and copies ran while one was open for 1% of the time, Pallas kernels for 7%

profile of v3, /device:TPU:32, one launch (start us, length us, event | category | flops | bytes accessed | tf_op | source)
XLA Modules:
  0.0 148.0 jit_solution(17103516112569194498)
XLA Ops:
  0.6 11.6 %all-to-all-start = ((f32[64,8,512]{2,1,0:T(8,128)}), f32[64,8,512]{2,1,0:T(8,128)S(1)}, u32[]{:S(2)}, u32[]{:S(2)}) async-start(f32[64,8,512]{2,1,0:T(8,128)} %bitcast.21), calls=%async_computation | async-start | bytes 2097152 | tf_op jit(solution)/shard_map/all_to_all | solution.py:173
  13.6 26.5 %all-to-all-done.q_ref = f32[64,8,512]{2,1,0:T(8,128)S(1)} async-done(((f32[64,8,512]{2,1,0:T(8,128)}), f32[64,8,512]{2,1,0:T(8,128)S(1)}, u32[]{:S(2)}, u32[]{:S(2)}) %all-to-all-start) | async-done | bytes 1048608 | tf_op jit(solution)/shard_map/all_to_all | solution.py:173
  42.8 10.3 %all-to-all-start.1 = ((f32[128,1,128]{2,1,0:T(1,128)}), f32[128,1,128]{2,1,0:T(1,128)S(1)}, u32[]{:S(2)}, u32[]{:S(2)}) async-start(f32[128,1,128]{2,1,0:T(1,128)} %broadcast_in_dim.25), calls=%async_computation.1 | async-start | bytes 131072 | tf_op jit(solution)/shard_map/all_to_all | solution.py:173
  53.2 10.9 %all-to-all-done.1.gathered_ref = f32[128,1,128]{2,1,0:T(1,128)S(1)} async-done(((f32[128,1,128]{2,1,0:T(1,128)}), f32[128,1,128]{2,1,0:T(1,128)S(1)}, u32[]{:S(2)}, u32[]{:S(2)}) %all-to-all-start.1) | async-done | bytes 65568 | tf_op jit(solution)/shard_map/all_to_all | solution.py:173
  64.9 1.2 collective-permute-done.1
  66.7 6.6 %all-to-all-start.2 = ((f32[128,1,128]{2,1,0:T(1,128)}), f32[128,1,128]{2,1,0:T(1,128)S(1)}, u32[]{:S(2)}, u32[]{:S(2)}) async-start(f32[128,1,128]{2,1,0:T(1,128)} %broadcast_in_dim.27), calls=%async_computation.2 | async-start | bytes 131072 | tf_op jit(solution)/shard_map/all_to_all | solution.py:173
  73.4 11.2 %all-to-all-done.2.gathered_ref = f32[128,1,128]{2,1,0:T(1,128)S(1)} async-done(((f32[128,1,128]{2,1,0:T(1,128)}), f32[128,1,128]{2,1,0:T(1,128)S(1)}, u32[]{:S(2)}, u32[]{:S(2)}) %all-to-all-start.2) | async-done | bytes 65568 | tf_op jit(solution)/shard_map/all_to_all | solution.py:173
  85.4 1.3 shard_map.71
  86.7 1.5 %collective-permute-start.10 = (s32[2,4,8,512]{3,2,1,0:T(8,128)}, s32[2,4,8,512]{3,2,1,0:T(8,128)S(1)}, u32[]{:S(2)}, u32[]{:S(2)}) collective-permute-start(s32[2,4,8,512]{3,2,1,0:T(8,128)} %get-tuple-element.41), channel_id=1, source_target_pairs={{0,48},{8,56},{16,0},{24,8},{32,16},{40,24},{48,32},{56,40},{1,49}... | collective-permute-start | bytes 393224 | tf_op jit(solution)/shard_map/ppermute | solution.py:178
  89.5 8.8 %all-to-all-start.3 = ((f32[128,1,128]{2,1,0:T(1,128)}), f32[128,1,128]{2,1,0:T(1,128)S(1)}, u32[]{:S(2)}, u32[]{:S(2)}) async-start(f32[128,1,128]{2,1,0:T(1,128)} %broadcast_in_dim.29), calls=%async_computation.3 | async-start | bytes 131072 | tf_op jit(solution)/shard_map/all_to_all | solution.py:173
  98.3 1.7 %collective-permute-start.5 = (s32[2,4,8,512]{3,2,1,0:T(8,128)S(1)}, s32[2,4,8,512]{3,2,1,0:T(8,128)S(1)}, u32[]{:S(2)}, u32[]{:S(2)}) collective-permute-start(s32[2,4,8,512]{3,2,1,0:T(8,128)S(1)} %get-tuple-element.36), channel_id=1, source_target_pairs={{0,8},{8,16},{16,24},{24,32},{32,40},{40,48},{48,56},{56,0},{1,9},... | collective-permute-start | bytes 393224 | tf_op jit(solution)/shard_map/ppermute | solution.py:178
  100.0 3.6 %collective-permute-start.6 = (s32[2,4,8,512]{3,2,1,0:T(8,128)S(1)}, s32[2,4,8,512]{3,2,1,0:T(8,128)S(1)}, u32[]{:S(2)}, u32[]{:S(2)}) collective-permute-start(s32[2,4,8,512]{3,2,1,0:T(8,128)S(1)} %get-tuple-element.37), channel_id=1, source_target_pairs={{0,16},{8,24},{16,32},{24,40},{32,48},{40,56},{48,0},{56,8},{1,17}... | collective-permute-start | bytes 393224 | tf_op jit(solution)/shard_map/ppermute | solution.py:178
  104.2 3.3 %collective-permute-start.8 = (s32[2,4,8,512]{3,2,1,0:T(8,128)S(1)}, s32[2,4,8,512]{3,2,1,0:T(8,128)S(1)}, u32[]{:S(2)}, u32[]{:S(2)}) collective-permute-start(s32[2,4,8,512]{3,2,1,0:T(8,128)S(1)} %get-tuple-element.39), channel_id=1, source_target_pairs={{0,32},{8,40},{16,48},{24,56},{32,0},{40,8},{48,16},{56,24},{1,33}... | collective-permute-start | bytes 393224 | tf_op jit(solution)/shard_map/ppermute | solution.py:178
  107.4 2.1 %collective-permute-start.9 = (s32[2,4,8,512]{3,2,1,0:T(8,128)S(1)}, s32[2,4,8,512]{3,2,1,0:T(8,128)S(1)}, u32[]{:S(2)}, u32[]{:S(2)}) collective-permute-start(s32[2,4,8,512]{3,2,1,0:T(8,128)S(1)} %get-tuple-element.40), channel_id=1, source_target_pairs={{0,40},{8,48},{16,56},{24,0},{32,8},{40,16},{48,24},{56,32},{1,41}... | collective-permute-start | bytes 393224 | tf_op jit(solution)/shard_map/ppermute | solution.py:178
  109.5 1.2 shard_map.70
  110.7 9.5 %all-to-all-start.4 = ((f32[32,1,1024]{2,1,0:T(1,128)}), f32[32,1,1024]{2,1,0:T(1,128)S(1)}, u32[]{:S(2)}, u32[]{:S(2)}) async-start(f32[32,1,1024]{2,1,0:T(1,128)} %get-tuple-element.34.back_ref), calls=%async_computation.4 | async-start | bytes 262144 | tf_op jit(solution)/shard_map/all_to_all | solution.py:173
  120.2 3.9 %collective-permute-done.7.refs_3_ = s32[2,4,8,512]{3,2,1,0:T(8,128)S(1)} collective-permute-done((s32[2,4,8,512]{3,2,1,0:T(8,128)S(1)}, s32[2,4,8,512]{3,2,1,0:T(8,128)S(1)}, u32[]{:S(2)}, u32[]{:S(2)}) %collective-permute-start.7) | collective-permute-done | bytes 131104 | tf_op jit(solution)/shard_map/ppermute | solution.py:178
  124.7 1.8 %collective-permute-start.12 = (s32[8,2,8,512]{3,2,1,0:T(8,128)S(1)}, s32[8,2,8,512]{3,2,1,0:T(8,128)S(1)}, u32[]{:S(2)}, u32[]{:S(2)}) collective-permute-start(s32[8,2,8,512]{3,2,1,0:T(8,128)S(1)} %get-tuple-element.44), channel_id=1, source_target_pairs={{0,64},{64,128},{128,192},{192,0},{1,65},{65,129},{129,193},{193,1... | collective-permute-start | bytes 786440 | tf_op jit(solution)/shard_map/ppermute | solution.py:178
  126.5 2.8 %collective-permute-start.13 = (s32[8,2,8,512]{3,2,1,0:T(8,128)S(1)}, s32[8,2,8,512]{3,2,1,0:T(8,128)S(1)}, u32[]{:S(2)}, u32[]{:S(2)}) collective-permute-start(s32[8,2,8,512]{3,2,1,0:T(8,128)S(1)} %get-tuple-element.45), channel_id=1, source_target_pairs={{0,128},{64,192},{128,0},{192,64},{1,129},{65,193},{129,1},{193,65... | collective-permute-start | bytes 786440 | tf_op jit(solution)/shard_map/ppermute | solution.py:178
  129.3 1.4 collective-permute-start.14
  131.0 3.3 %collective-permute-done.12.refs_1_ = s32[8,2,8,512]{3,2,1,0:T(8,128)S(1)} collective-permute-done((s32[8,2,8,512]{3,2,1,0:T(8,128)S(1)}, s32[8,2,8,512]{3,2,1,0:T(8,128)S(1)}, u32[]{:S(2)}, u32[]{:S(2)}) %collective-permute-start.12) | collective-permute-done | bytes 262176 | tf_op jit(solution)/shard_map/ppermute | solution.py:178
  134.3 5.9 %collective-permute-done.13.refs_2_ = s32[8,2,8,512]{3,2,1,0:T(8,128)S(1)} collective-permute-done((s32[8,2,8,512]{3,2,1,0:T(8,128)S(1)}, s32[8,2,8,512]{3,2,1,0:T(8,128)S(1)}, u32[]{:S(2)}, u32[]{:S(2)}) %collective-permute-start.13) | collective-permute-done | bytes 262176 | tf_op jit(solution)/shard_map/ppermute | solution.py:178
  140.9 5.3 %shard_map.73 = f32[18,512]{1,0:T(8,128)} custom-call(s32[3]{0:T(128)S(1)} %pad_add_fusion.at_ref, f32[64,8,512]{2,1,0:T(8,128)S(1)} %all-to-all-done.q_ref, f32[32,1,1024]{2,1,0:T(1,128)} %get-tuple-element.34.back_ref, f32[1,128]{1,0:T(1,128)S(1)} %copy-done.2, s32[8,2,8,512]{3,2,1,0:T(8,128)S(1)} %get-tuple-element.43.refs_0_, ...), custom_call_target="tpu_custom_call" | custom-call | flops 20000000 | bytes 2000000 | tf_op jit(solution)/shard_map/pallas_call | solution.py:231
  146.2 1.7 %weights.1 = f32[8,32768]{1,0:T(8,128)} custom-call(s32[3]{0:T(128)S(1)} %pad_add_fusion.at_ref, f32[1,128]{1,0:T(1,128)S(1)} %copy-done.2, f32[8,32768]{1,0:T(8,128)S(1)} %copy-done, f32[32,1,1024]{2,1,0:T(1,128)S(1)} %all-to-all-done.4.same_ref, f32[32,1,1024]{2,1,0:T(1,128)S(1)} %collective-permute-done.3.other_ref), custom_call_target="tpu_custom_call" | custom-call | flops 1000000 | bytes 2000000 | tf_op jit(solution)/shard_map/weights/pallas_call | solution.py:236
  (38 shorter events, 8.5 us)
Async XLA Ops:
  0.6 39.5 %all-to-all-start = ((f32[64,8,512]{2,1,0:T(8,128)}), f32[64,8,512]{2,1,0:T(8,128)S(1)}, u32[]{:S(2)}, u32[]{:S(2)}) async-start(f32[64,8,512]{2,1,0:T(8,128)} %bitcast.21), calls=%async_computation | async-start | bytes 2097152 | tf_op jit(solution)/shard_map/all_to_all | solution.py:173
  12.2 40.8 %copy-start.1 = (s32[8,32768]{1,0:T(8,128)S(1)}, s32[8,32768]{1,0:T(8,128)}, u32[]{:S(2)}) copy-start(s32[8,32768]{1,0:T(8,128)} %param.5) | copy-start | bytes 3145732
  40.9 1.2 collective-permute-start
  42.8 21.4 %all-to-all-start.1 = ((f32[128,1,128]{2,1,0:T(1,128)}), f32[128,1,128]{2,1,0:T(1,128)S(1)}, u32[]{:S(2)}, u32[]{:S(2)}) async-start(f32[128,1,128]{2,1,0:T(1,128)} %broadcast_in_dim.25), calls=%async_computation.1 | async-start | bytes 131072 | tf_op jit(solution)/shard_map/all_to_all | solution.py:173
  53.1 32.3 %collective-permute-start.4 = (s32[4,8,8,512]{3,2,1,0:T(8,128)S(1)}, s32[4,8,8,512]{3,2,1,0:T(8,128)S(1)}, u32[]{:S(2)}, u32[]{:S(2)}) collective-permute-start(s32[4,8,8,512]{3,2,1,0:T(8,128)S(1)} %dynamic-slice_bitcast_fusion), channel_id=1, source_target_pairs={{0,4},{4,0},{1,5},{5,1},{2,6},{6,2},{3,7},{7,3},{8,12},{12,8},{9,1... | collective-permute-start | bytes 1572872 | tf_op jit(solution)/shard_map/ppermute | solution.py:178
  64.9 1.2 collective-permute-start.1
  66.7 17.8 %all-to-all-start.2 = ((f32[128,1,128]{2,1,0:T(1,128)}), f32[128,1,128]{2,1,0:T(1,128)S(1)}, u32[]{:S(2)}, u32[]{:S(2)}) async-start(f32[128,1,128]{2,1,0:T(1,128)} %broadcast_in_dim.27), calls=%async_computation.2 | async-start | bytes 131072 | tf_op jit(solution)/shard_map/all_to_all | solution.py:173
  85.4 3.5 %collective-permute-start.2 = (f32[1,128]{1,0:T(1,128)S(1)}, f32[1,128]{1,0:T(1,128)S(1)}, u32[]{:S(2)}, u32[]{:S(2)}) collective-permute-start(f32[1,128]{1,0:T(1,128)S(1)} %get-tuple-element.32), channel_id=1, source_target_pairs={{0,4},{4,0},{1,5},{5,1},{2,6},{6,2},{3,7},{7,3},{8,12},{12,8},{9,1... | collective-permute-start | bytes 1544 | tf_op jit(solution)/shard_map/ppermute | solution.py:178
  86.7 17.4 %collective-permute-start.10 = (s32[2,4,8,512]{3,2,1,0:T(8,128)}, s32[2,4,8,512]{3,2,1,0:T(8,128)S(1)}, u32[]{:S(2)}, u32[]{:S(2)}) collective-permute-start(s32[2,4,8,512]{3,2,1,0:T(8,128)} %get-tuple-element.41), channel_id=1, source_target_pairs={{0,48},{8,56},{16,0},{24,8},{32,16},{40,24},{48,32},{56,40},{1,49}... | collective-permute-start | bytes 393224 | tf_op jit(solution)/shard_map/ppermute | solution.py:178
  88.3 19.2 %collective-permute-start.11 = (s32[2,4,8,512]{3,2,1,0:T(8,128)S(1)}, s32[2,4,8,512]{3,2,1,0:T(8,128)S(1)}, u32[]{:S(2)}, u32[]{:S(2)}) collective-permute-start(s32[2,4,8,512]{3,2,1,0:T(8,128)S(1)} %get-tuple-element.42), channel_id=1, source_target_pairs={{0,56},{8,0},{16,8},{24,16},{32,24},{40,32},{48,40},{56,48},{1,57}... | collective-permute-start | bytes 393224 | tf_op jit(solution)/shard_map/ppermute | solution.py:178
  89.5 20.0 %all-to-all-start.3 = ((f32[128,1,128]{2,1,0:T(1,128)}), f32[128,1,128]{2,1,0:T(1,128)S(1)}, u32[]{:S(2)}, u32[]{:S(2)}) async-start(f32[128,1,128]{2,1,0:T(1,128)} %broadcast_in_dim.29), calls=%async_computation.3 | async-start | bytes 131072 | tf_op jit(solution)/shard_map/all_to_all | solution.py:173
  98.3 21.9 %collective-permute-start.5 = (s32[2,4,8,512]{3,2,1,0:T(8,128)S(1)}, s32[2,4,8,512]{3,2,1,0:T(8,128)S(1)}, u32[]{:S(2)}, u32[]{:S(2)}) collective-permute-start(s32[2,4,8,512]{3,2,1,0:T(8,128)S(1)} %get-tuple-element.36), channel_id=1, source_target_pairs={{0,8},{8,16},{16,24},{24,32},{32,40},{40,48},{48,56},{56,0},{1,9},... | collective-permute-start | bytes 393224 | tf_op jit(solution)/shard_map/ppermute | solution.py:178
  100.0 20.2 %collective-permute-start.6 = (s32[2,4,8,512]{3,2,1,0:T(8,128)S(1)}, s32[2,4,8,512]{3,2,1,0:T(8,128)S(1)}, u32[]{:S(2)}, u32[]{:S(2)}) collective-permute-start(s32[2,4,8,512]{3,2,1,0:T(8,128)S(1)} %get-tuple-element.37), channel_id=1, source_target_pairs={{0,16},{8,24},{16,32},{24,40},{32,48},{40,56},{48,0},{56,8},{1,17}... | collective-permute-start | bytes 393224 | tf_op jit(solution)/shard_map/ppermute | solution.py:178
  103.6 20.5 %collective-permute-start.7 = (s32[2,4,8,512]{3,2,1,0:T(8,128)S(1)}, s32[2,4,8,512]{3,2,1,0:T(8,128)S(1)}, u32[]{:S(2)}, u32[]{:S(2)}) collective-permute-start(s32[2,4,8,512]{3,2,1,0:T(8,128)S(1)} %get-tuple-element.38), channel_id=1, source_target_pairs={{0,24},{8,32},{16,40},{24,48},{32,56},{40,0},{48,8},{56,16},{1,25}... | collective-permute-start | bytes 393224 | tf_op jit(solution)/shard_map/ppermute | solution.py:178
  104.2 19.9 %collective-permute-start.8 = (s32[2,4,8,512]{3,2,1,0:T(8,128)S(1)}, s32[2,4,8,512]{3,2,1,0:T(8,128)S(1)}, u32[]{:S(2)}, u32[]{:S(2)}) collective-permute-start(s32[2,4,8,512]{3,2,1,0:T(8,128)S(1)} %get-tuple-element.39), channel_id=1, source_target_pairs={{0,32},{8,40},{16,48},{24,56},{32,0},{40,8},{48,16},{56,24},{1,33}... | collective-permute-start | bytes 393224 | tf_op jit(solution)/shard_map/ppermute | solution.py:178
  107.4 16.7 %collective-permute-start.9 = (s32[2,4,8,512]{3,2,1,0:T(8,128)S(1)}, s32[2,4,8,512]{3,2,1,0:T(8,128)S(1)}, u32[]{:S(2)}, u32[]{:S(2)}) collective-permute-start(s32[2,4,8,512]{3,2,1,0:T(8,128)S(1)} %get-tuple-element.40), channel_id=1, source_target_pairs={{0,40},{8,48},{16,56},{24,0},{32,8},{40,16},{48,24},{56,32},{1,41}... | collective-permute-start | bytes 393224 | tf_op jit(solution)/shard_map/ppermute | solution.py:178
  110.7 20.2 %all-to-all-start.4 = ((f32[32,1,1024]{2,1,0:T(1,128)}), f32[32,1,1024]{2,1,0:T(1,128)S(1)}, u32[]{:S(2)}, u32[]{:S(2)}) async-start(f32[32,1,1024]{2,1,0:T(1,128)} %get-tuple-element.34.back_ref), calls=%async_computation.4 | async-start | bytes 262144 | tf_op jit(solution)/shard_map/all_to_all | solution.py:173
  124.7 9.6 %collective-permute-start.12 = (s32[8,2,8,512]{3,2,1,0:T(8,128)S(1)}, s32[8,2,8,512]{3,2,1,0:T(8,128)S(1)}, u32[]{:S(2)}, u32[]{:S(2)}) collective-permute-start(s32[8,2,8,512]{3,2,1,0:T(8,128)S(1)} %get-tuple-element.44), channel_id=1, source_target_pairs={{0,64},{64,128},{128,192},{192,0},{1,65},{65,129},{129,193},{193,1... | collective-permute-start | bytes 786440 | tf_op jit(solution)/shard_map/ppermute | solution.py:178
  126.5 13.7 %collective-permute-start.13 = (s32[8,2,8,512]{3,2,1,0:T(8,128)S(1)}, s32[8,2,8,512]{3,2,1,0:T(8,128)S(1)}, u32[]{:S(2)}, u32[]{:S(2)}) collective-permute-start(s32[8,2,8,512]{3,2,1,0:T(8,128)S(1)} %get-tuple-element.45), channel_id=1, source_target_pairs={{0,128},{64,192},{128,0},{192,64},{1,129},{65,193},{129,1},{193,65... | collective-permute-start | bytes 786440 | tf_op jit(solution)/shard_map/ppermute | solution.py:178
  129.3 10.9 %collective-permute-start.14 = (s32[8,2,8,512]{3,2,1,0:T(8,128)S(1)}, s32[8,2,8,512]{3,2,1,0:T(8,128)S(1)}, u32[]{:S(2)}, u32[]{:S(2)}) collective-permute-start(s32[8,2,8,512]{3,2,1,0:T(8,128)S(1)} %get-tuple-element.46), channel_id=1, source_target_pairs={{0,192},{64,0},{128,64},{192,128},{1,193},{65,1},{129,65},{193,129... | collective-permute-start | bytes 786440 | tf_op jit(solution)/shard_map/ppermute | solution.py:178
  131.0 15.2 %collective-permute-start.3 = (f32[32,1,1024]{2,1,0:T(1,128)S(1)}, f32[32,1,1024]{2,1,0:T(1,128)S(1)}, u32[]{:S(2)}, u32[]{:S(2)}) collective-permute-start(f32[32,1,1024]{2,1,0:T(1,128)S(1)} %all-to-all-done.4.same_ref), channel_id=1, source_target_pairs={{0,4},{4,0},{1,5},{5,1},{2,6},{6,2},{3,7},{7,3},{8,12},{12,8},{9,1... | collective-permute-start | bytes 393224 | tf_op jit(solution)/shard_map/ppermute | solution.py:178
  140.2 0.7 copy-start.2
  140.9 5.3 %copy-start = (f32[8,32768]{1,0:T(8,128)S(1)}, f32[8,32768]{1,0:T(8,128)}, u32[]{:S(2)}) copy-start(f32[8,32768]{1,0:T(8,128)} %x_ref.1) | copy-start | bytes 3145732
